TPU v7x, 32 devices: a whole 2x2x4 slice. The times are simulated.
32 devices in a mesh: data: 4 (over z), col: 2 (over y), row: 4 (over x, core).
Axes of the slice: x: 2, y: 2, z: 4, core: 2. Of those that a mesh axis runs over, the one named last changes fastest.
Arguments:
- x_in: bfloat16 [2048, 2048], P(None, 'row')
- h_act: bfloat16 [2048, 5632], P(None, 'row')
- d_gate: bfloat16 [2048, 5632], P(None, 'col')
- d_up: bfloat16 [2048, 5632], P(None, 'col')
- d_out: bfloat16 [2048, 2048], P(None, 'col')
- w_gate: float32 [2048, 5632], P('row', 'col')
- w_up: float32 [2048, 5632], P('row', 'col')
- w_down: float32 [5632, 2048], P('row', 'col')
- r_gate: float32 [2048], P('row')
- c_gate: float32 [5632], P('col')
- r_up: float32 [2048], P('row')
- c_up: float32 [5632], P('col')
- r_down: float32 [5632], P('row')
- c_down: float32 [2048], P('col')
- beta_two: float32 [], replicated
- rel_step: float32 [], replicated
- clip_thr: float32 [], replicated
Outputs:
- output 1: float32 [2048, 5632], P('row', 'col')
- output 2: float32 [2048, 5632], P('row', 'col')
- output 3: float32 [5632, 2048], P('row', 'col')
- output 4: float32 [2048], P('row')
- output 5: float32 [5632], P('col')
- output 6: float32 [2048], P('row')
- output 7: float32 [5632], P('col')
- output 8: float32 [5632], P('row')
- output 9: float32 [2048], P('col')
All inputs are finite; a program needn't handle non-finite values.
Results may differ from a plain program's by a relative error of at most 0.001.
Values are sent between devices in bfloat16 or wider.
A program may use at most 1 GiB of HBM per device.

v0:
```python
import jax
import jax.numpy as jnp
from jax import lax
from jax.sharding import PartitionSpec as P

EPS_SQ = 1e-30
EPS_SCALE = 1e-3
CONTRACT_TOKENS = (((0,), (0,)), ((), ()))


def solution(mesh):
    row_count = mesh.shape["row"]
    col_count = mesh.shape["col"]

    def block_step(w_blk, act_in, cot_out, r_old, c_old, beta_two, rel_step, clip_thr):
        g_blk = lax.dot_general(act_in, cot_out, CONTRACT_TOKENS, preferred_element_type=jnp.float32)
        m_total = g_blk.shape[0] * row_count
        n_total = g_blk.shape[1] * col_count
        q_blk = g_blk * g_blk + EPS_SQ
        row_sum = lax.psum(jnp.sum(q_blk, axis=1), "col")
        col_sum = lax.psum(jnp.sum(q_blk, axis=0), "row")
        r_new = beta_two * r_old + (1.0 - beta_two) * (row_sum / n_total)
        c_new = beta_two * c_old + (1.0 - beta_two) * (col_sum / m_total)
        r_mean = lax.psum(jnp.sum(r_new), "row") / m_total
        u_blk = g_blk / jnp.sqrt(r_new[:, None] * c_new[None, :] / r_mean)
        u_rms = jnp.sqrt(lax.psum(jnp.sum(u_blk * u_blk), ("row", "col")) / (m_total * n_total))
        w_rms = jnp.sqrt(lax.psum(jnp.sum(w_blk * w_blk), ("row", "col")) / (m_total * n_total))
        u_hat = u_blk / jnp.maximum(1.0, u_rms / clip_thr)
        step_size = rel_step * jnp.maximum(EPS_SCALE, w_rms)
        return w_blk - step_size * u_hat, r_new, c_new

    def local_program(x_in, h_act, d_gate, d_up, d_out, w_gate, w_up, w_down, r_gate, c_gate, r_up, c_up, r_down, c_down, beta_two, rel_step, clip_thr):
        gate_out = block_step(w_gate, x_in, d_gate, r_gate, c_gate, beta_two, rel_step, clip_thr)
        up_out = block_step(w_up, x_in, d_up, r_up, c_up, beta_two, rel_step, clip_thr)
        down_out = block_step(w_down, h_act, d_out, r_down, c_down, beta_two, rel_step, clip_thr)
        return (gate_out[0], up_out[0], down_out[0], gate_out[1], gate_out[2], up_out[1], up_out[2], down_out[1], down_out[2])

    act_spec = P(None, "row")
    cot_spec = P(None, "col")
    w_spec = P("row", "col")
    r_spec = P("row")
    c_spec = P("col")
    s_spec = P()
    return jax.shard_map(local_program, mesh=mesh, in_specs=(act_spec, act_spec, cot_spec, cot_spec, cot_spec, w_spec, w_spec, w_spec, r_spec, c_spec, r_spec, c_spec, r_spec, c_spec, s_spec, s_spec, s_spec), out_specs=(w_spec, w_spec, w_spec, r_spec, c_spec, r_spec, c_spec, r_spec, c_spec), check_vma=False)
```

profile of v0, /device:TPU:0, one launch (start us, length us, event | category | flops | bytes accessed | tf_op | source)
XLA Modules:
  0.0 114.2 jit_solution(16245887481946724602)
XLA Ops:
  0.6 0.0 copy-start
  2.8 0.0 copy-start.2
  2.8 4.9 %multiply_reduce_fusion.1 = f32[]{:T(128)} fusion(f32[1408,1024]{1,0:T(8,128)} %param.24), kind=kLoop, calls=%fused_computation.4 | loop fusion | flops 2883583 | bytes 5767172 | tf_op jit(solution)/shard_map/reduce_sum | solution.py:27
  7.7 5.6 %multiply_reduce_fusion.3 = (f32[]{:T(128)}, f32[]{:T(128)}) fusion(f32[512,2816]{1,0:T(8,128)} %param.23, f32[512,2816]{1,0:T(8,128)S(1)} %copy-done.2), kind=kLoop, calls=%fused_computation.9 | loop fusion | flops 5767166 | bytes 11534344 | tf_op jit(solution)/shard_map/reduce_sum | solution.py:27
  13.3 8.5 %fusion.4 = (f32[1024]{0:T(1024)S(1)}, f32[1408]{0:T(1024)S(1)}, f32[1408,1024]{1,0:T(8,128)}) fusion(bf16[2048,1408]{1,0:T(8,128)(2,1)S(1)} %copy-done.16, bf16[2048,1024]{1,0:T(8,128)(2,1)S(1)} %copy-done.17), kind=kOutput, calls=%fused_computation.19 | convolution fusion | flops 5911344640 | bytes 15738368 | tf_op jit(solution)/shard_map/dot_general | solution.py:16
  21.8 8.4 %fusion = (f32[2816]{0:T(1024)S(1)}, f32[512]{0:T(512)S(1)}, f32[512,2816]{1,0:T(8,128)}) fusion(bf16[2048,512]{1,0:T(8,128)(2,1)S(1)} %copy-done, bf16[2048,2816]{1,0:T(8,128)(2,1)S(1)} %bitcast.11), kind=kOutput, calls=%fused_computation.15 | convolution fusion | flops 5911343616 | bytes 19411968 | tf_op jit(solution)/shard_map/dot_general | solution.py:16
  30.2 11.5 %fusion.2 = (f32[2816]{0:T(1024)S(1)}, f32[512]{0:T(512)S(1)}, f32[512,2816]{1,0:T(8,128)}) fusion(bf16[2048,512]{1,0:T(8,128)(2,1)S(1)} %copy-done, bf16[2048,2816]{1,0:T(8,128)(2,1)} %param.20), kind=kOutput, calls=%fused_computation.17 | convolution fusion | flops 5911343616 | bytes 19411968 | tf_op jit(solution)/shard_map/dot_general | solution.py:16
  41.7 9.8 %all-reduce.2 = (f32[512]{0:T(512)S(1)}, f32[512]{0:T(512)S(1)}, f32[1408]{0:T(1024)S(1)}) all-reduce(f32[512]{0:T(512)S(1)} %get-tuple-element.14, f32[512]{0:T(512)S(1)} %get-tuple-element.12, f32[1408]{0:T(1024)S(1)} %get-tuple-element.10), channel_id=1, replica_groups=mesh['data'=4,'col'=2,'row'=4] {'col'}, use_global_device_ids=true, to_apply=%region_3.0 | all-reduce | flops 2432 | bytes 19456 | tf_op jit(solution)/shard_map/psum | solution.py:20
  51.5 0.6 fusion.7
  52.2 0.6 fusion.6
  52.8 11.5 %all-reduce.1 = (f32[]{:T(128)}, f32[2816]{0:T(1024)S(1)}, f32[]{:T(128)}, f32[2816]{0:T(1024)S(1)}, f32[]{:T(128)}, /*index=5*/f32[1024]{0:T(1024)S(1)}) all-reduce(f32[]{:T(128)} %get-tuple-element.39, f32[2816]{0:T(1024)S(1)} %get-tuple-element.13, f32[]{:T(128)} %get-tuple-element.32, ...), channel_id=1, replica_groups=mesh['data'=4,'col'=2,'row'=4] {'row'}, use_global_device_ids=true, to_apply=%region_7.0 | all-reduce | flops 6659 | bytes 53272 | tf_op jit(solution)/shard_map/psum | solution.py:24
  66.2 0.0 copy-start.4
  66.3 0.0 copy-start.11
  66.3 0.0 copy-start.3
  66.3 5.0 %multiply_reduce_fusion.4 = f32[]{:T(128)} fusion(f32[512,2816]{1,0:T(8,128)} %get-tuple-element.36, f32[]{:T(128)S(6)} %div.90, f32[2816]{0:T(1024)S(1)} %multiply_add_fusion.4, f32[512]{0:T(512)S(1)} %get-tuple-element.40), kind=kLoop, calls=%fused_computation.11 | loop fusion | flops 7208959 | bytes 5780488 | tf_op jit(solution)/shard_map/reduce_sum | solution.py:26
  71.2 4.9 %multiply_reduce_fusion = f32[]{:T(128)} fusion(f32[1408,1024]{1,0:T(8,128)} %get-tuple-element.38, f32[]{:T(128)S(6)} %div.108, f32[1024]{0:T(1024)S(1)} %multiply_add_fusion.6, f32[1408]{0:T(1024)S(1)} %get-tuple-element.31), kind=kLoop, calls=%fused_computation.1 | loop fusion | flops 7208959 | bytes 5776904 | tf_op jit(solution)/shard_map/reduce_sum | solution.py:26
  76.1 0.0 copy-start.5
  76.1 2.6 %multiply_reduce_fusion.2 = f32[]{:T(128)} fusion(f32[512,2816]{1,0:T(8,128)S(1)} %copy-done.3, f32[]{:T(128)S(6)} %div.99, f32[2816]{0:T(1024)S(1)} %multiply_add_fusion.3, f32[512]{0:T(512)S(1)} %get-tuple-element.33), kind=kLoop, calls=%fused_computation.6 | loop fusion | flops 7208959 | bytes 5780488 | tf_op jit(solution)/shard_map/reduce_sum | solution.py:26
  78.7 12.6 %all-reduce = (f32[]{:T(128)}, f32[]{:T(128)}, f32[]{:T(128)}, f32[]{:T(128)}, f32[]{:T(128)}, /*index=5*/f32[]{:T(128)}) all-reduce(f32[]{:T(128)} %multiply_reduce_fusion.4, f32[]{:T(128)} %get-tuple-element.42, f32[]{:T(128)} %multiply_reduce_fusion.2, ...), channel_id=1, replica_groups=mesh['data'=4,'col'=2,'row'=4] {'row','col'}, use_global_device_ids=true, to_apply=%region_9.0 | all-reduce | flops 6 | bytes 48 | tf_op jit(solution)/shard_map/psum | solution.py:26
  95.6 0.0 slice-start
  95.6 6.8 %multiply_subtract_fusion.2 = f32[512,2816]{1,0:T(8,128)} fusion(f32[512,2816]{1,0:T(8,128)} %param.22, f32[]{:T(128)S(6)} %max.19, f32[]{:T(128)S(6)} %mul.162, f32[512,2816]{1,0:T(8,128)} %get-tuple-element.36, f32[]{:T(128)S(6)} %div.90, f32[2816]{0:T(1024)S(1)} %multiply_add_fusion.4, f32[512]{0:T(512)S(1)} %get-tuple-element.40), kind=kLoop, calls=%fused_computation.10 | loop fusion | flops 8650752 | bytes 17314828 | tf_op jit(solution)/shard_map/sub | solution.py:30
  102.4 7.5 %multiply_subtract_fusion.1 = f32[512,2816]{1,0:T(8,128)} fusion(f32[512,2816]{1,0:T(8,128)} %param.23, f32[]{:T(128)S(6)} %max.21, f32[]{:T(128)S(6)} %mul.181, f32[512,2816]{1,0:T(8,128)} %get-tuple-element.37, f32[]{:T(128)S(6)} %div.99, f32[2816]{0:T(1024)S(1)} %multiply_add_fusion.3, f32[512]{0:T(512)S(1)} %get-tuple-element.33), kind=kLoop, calls=%fused_computation.5 | loop fusion | flops 8650752 | bytes 17314828 | tf_op jit(solution)/shard_map/sub | solution.py:30
  110.0 0.8 slice-done.3
  110.8 3.4 %multiply_subtract_fusion = f32[1408,1024]{1,0:T(8,128)} fusion(f32[1408,1024]{1,0:T(8,128)S(1)} %bitcast.7, f32[]{:T(128)S(6)} %max.23, f32[]{:T(128)S(6)} %mul.194, f32[1408,1024]{1,0:T(8,128)S(1)} %bitcast.9, f32[]{:T(128)S(6)} %div.108, f32[1024]{0:T(1024)S(1)} %multiply_add_fusion.6, f32[1408]{0:T(1024)S(1)} %get-tuple-element.31), kind=kLoop, calls=%fused_computation | loop fusion | flops 8650752 | bytes 17311244 | tf_op jit(solution)/shard_map/sub | solution.py:30
  (48 shorter events, 0.1 us)
Async XLA Ops:
  0.6 21.2 %copy-start = (bf16[2048,512]{1,0:T(8,128)(2,1)S(1)}, bf16[2048,512]{1,0:T(8,128)(2,1)}, u32[]{:S(2)}) copy-start(bf16[2048,512]{1,0:T(8,128)(2,1)} %param.17) | copy-start | bytes 6291460
  2.8 10.5 %copy-start.16 = (bf16[2048,1408]{1,0:T(8,128)(2,1)S(1)}, bf16[2048,1408]{1,0:T(8,128)(2,1)}, u32[]{:S(2)}) copy-start(bf16[2048,1408]{1,0:T(8,128)(2,1)} %param.18) | copy-start | bytes 17301508
  2.8 10.5 %copy-start.17 = (bf16[2048,1024]{1,0:T(8,128)(2,1)S(1)}, bf16[2048,1024]{1,0:T(8,128)(2,1)}, u32[]{:S(2)}) copy-start(bf16[2048,1024]{1,0:T(8,128)(2,1)} %param.21) | copy-start | bytes 12582916
  7.7 14.1 %slice-start.4 = ((s8[11534336]{0:T(1024)(128)(4,1)}), s8[3145728]{0:T(1024)(128)(4,1)S(1)}, s32[]{:S(2)}) async-start(s8[11534336]{0:T(1024)(128)(4,1)} %bitcast.10), calls=%async_computation.4 | async-start | bytes 6291456
  7.7 14.1 %slice-start.5 = ((s8[11534336]{0:T(1024)(128)(4,1)}), s8[4194304]{0:T(1024)(128)(4,1)S(1)}, s32[]{:S(2)}) async-start(s8[11534336]{0:T(1024)(128)(4,1)} %bitcast.10), calls=%async_computation.5 | async-start | bytes 8388608
  13.3 8.5 %slice-start.6 = ((s8[11534336]{0:T(1024)(128)(4,1)}), s8[4194304]{0:T(1024)(128)(4,1)S(1)}, s32[]{:S(2)}) async-start(s8[11534336]{0:T(1024)(128)(4,1)} %bitcast.10), calls=%async_computation.6 | async-start | bytes 8388608
  30.2 21.3 %copy-start.14 = (f32[512]{0:T(512)S(1)}, f32[512]{0:T(512)}, u32[]{:S(2)}) copy-start(f32[512]{0:T(512)} %param.27) | copy-start | bytes 6148
  30.2 21.3 %copy-start.15 = (f32[512]{0:T(512)S(1)}, f32[512]{0:T(512)}, u32[]{:S(2)}) copy-start(f32[512]{0:T(512)} %param.25) | copy-start | bytes 6148
  30.2 22.0 %copy-start.12 = (f32[1408]{0:T(1024)S(1)}, f32[1408]{0:T(1024)}, u32[]{:S(2)}) copy-start(f32[1408]{0:T(1024)} %param.29) | copy-start | bytes 16900
  30.2 36.0 %copy-start.10 = (f32[2816]{0:T(1024)S(1)}, f32[2816]{0:T(1024)}, u32[]{:S(2)}) copy-start(f32[2816]{0:T(1024)} %param.26) | copy-start | bytes 33796
  41.7 29.5 %copy-start.13 = (f32[1024]{0:T(1024)S(1)}, f32[1024]{0:T(1024)}, u32[]{:S(2)}) copy-start(f32[1024]{0:T(1024)} %param.30) | copy-start | bytes 12292
  52.2 43.4 %copy-start.9 = (f32[512]{0:T(512)}, f32[512]{0:T(512)S(1)}, u32[]{:S(2)}) copy-start(f32[512]{0:T(512)S(1)} %get-tuple-element.40) | copy-start | bytes 6148
  52.2 50.2 %copy-start.8 = (f32[512]{0:T(512)}, f32[512]{0:T(512)S(1)}, u32[]{:S(2)}) copy-start(f32[512]{0:T(512)S(1)} %get-tuple-element.33) | copy-start | bytes 6148
  52.8 57.2 %copy-start.6 = (f32[1408]{0:T(1024)}, f32[1408]{0:T(1024)S(1)}, u32[]{:S(2)}) copy-start(f32[1408]{0:T(1024)S(1)} %get-tuple-element.31) | copy-start | bytes 16900
  66.2 29.3 %copy-start.4 = (f32[2816]{0:T(1024)}, f32[2816]{0:T(1024)S(1)}, u32[]{:S(2)}) copy-start(f32[2816]{0:T(1024)S(1)} %multiply_add_fusion.4) | copy-start | bytes 33796
  66.3 9.8 %copy-start.11 = (f32[2816]{0:T(1024)S(1)}, f32[2816]{0:T(1024)}, u32[]{:S(2)}) copy-start(f32[2816]{0:T(1024)} %param.28) | copy-start | bytes 33796
  66.3 9.8 %copy-start.3 = (f32[512,2816]{1,0:T(8,128)S(1)}, f32[512,2816]{1,0:T(8,128)}, u32[]{:S(2)}) copy-start(f32[512,2816]{1,0:T(8,128)} %get-tuple-element.37) | copy-start | bytes 17301508
  71.2 38.7 %copy-start.7 = (f32[1024]{0:T(1024)}, f32[1024]{0:T(1024)S(1)}, u32[]{:S(2)}) copy-start(f32[1024]{0:T(1024)S(1)} %multiply_add_fusion.6) | copy-start | bytes 12292
  76.1 26.3 %copy-start.5 = (f32[2816]{0:T(1024)}, f32[2816]{0:T(1024)S(1)}, u32[]{:S(2)}) copy-start(f32[2816]{0:T(1024)S(1)} %multiply_add_fusion.3) | copy-start | bytes 33796
  95.6 14.4 %slice-start = ((s8[5767168]{0:T(1024)(128)(4,1)}), s8[4194304]{0:T(1024)(128)(4,1)S(1)}, s32[]{:S(2)}) async-start(s8[5767168]{0:T(1024)(128)(4,1)} %bitcast.6), calls=%async_computation | async-start | bytes 8388608
  95.6 14.4 %slice-start.2 = ((s8[5767168]{0:T(1024)(128)(4,1)}), s8[4194304]{0:T(1024)(128)(4,1)S(1)}, s32[]{:S(2)}) async-start(s8[5767168]{0:T(1024)(128)(4,1)} %bitcast.8), calls=%async_computation.2 | async-start | bytes 8388608
  102.4 7.5 %slice-start.1 = ((s8[5767168]{0:T(1024)(128)(4,1)}), s8[1572864]{0:T(1024)(128)(4,1)S(1)}, s32[]{:S(2)}) async-start(s8[5767168]{0:T(1024)(128)(4,1)} %bitcast.6), calls=%async_computation.1 | async-start | bytes 3145728
  102.4 8.4 %slice-start.3 = ((s8[5767168]{0:T(1024)(128)(4,1)}), s8[1572864]{0:T(1024)(128)(4,1)S(1)}, s32[]{:S(2)}) async-start(s8[5767168]{0:T(1024)(128)(4,1)} %bitcast.8), calls=%async_computation.3 | async-start | bytes 3145728
  102.4 11.8 %copy-start.1 = (bf16[2048,512]{1,0:T(8,128)(2,1)S(1)}, bf16[2048,512]{1,0:T(8,128)(2,1)}, u32[]{:S(2)}) copy-start(bf16[2048,512]{1,0:T(8,128)(2,1)} %param.17) | copy-start | bytes 6291460
  (1 other events, 4.9 us)
where the time goes:
time: 115 us; the launch traced here: 114 us
  other arithmetic  41.9 us (36%)
  blocking collectives  33.9 us (29%)
  matrix products  28.4 us (25%)
  between operations  9.06 us (8%)
    dot_general x3, matrix products, block_step(): lax.dot_general(act_in, cot_out, CONTRACT_TOKENS, preferred_element_type=...  28.4 us
    sub x3, other arithmetic, block_step(): return (w_blk - step_size * u_hat, r_new, c_new)  17.7 us
    psum x1, blocking collectives, block_step(): lax.psum(jnp.sum(u_blk * u_blk), ('row', 'col')) / (m_total * n_total)  12.6 us
    reduce_sum x3, other arithmetic, block_step(): jnp.sum(u_blk * u_blk)  12.4 us
    psum x1, blocking collectives, block_step(): r_mean = lax.psum(jnp.sum(r_new), 'row') / m_total  11.5 us
    reduce_sum x2, other arithmetic, block_step(): jnp.sum(w_blk * w_blk)  10.5 us
    psum x1, blocking collectives, block_step(): row_sum = lax.psum(jnp.sum(q_blk, axis=1), 'col')  9.81 us

commit v1 on v0

v1 whole, which is shorter than its diff:
```python
import functools

import jax
import jax.numpy as jnp
from jax import lax
from jax.experimental import pallas as pl
from jax.experimental.pallas import tpu as pltpu
from jax.sharding import PartitionSpec as P

EPS_SQ = 1e-30
EPS_SCALE = 1e-3
F32 = jnp.float32
BF16 = jnp.bfloat16
MESH = pl.DeviceIdType.MESH
VM = pltpu.VMEM
HB = pltpu.HBM
KB = 256
NT = 256
RING = 8
PIECES = (176, 80, 96)


def block_rows(q, w, c, dims):
    first = 0
    for m, n in (tuple(dims) + tuple(dims))[:q + 3 * w]:
        first += m * (n // 128)
    return first + c * dims[q][0]


def dot_kernel(
    dims,
    x, h, dg, du, dd, wg, wu, wd, rg, cg, ru, cu, rd, cd,
    held, rs_g, rs_u, rs_d, cs_g, cs_u, cs_d, sw, ro, co,
    xs, hs, xt, ht, ring, x_sem, h_sem, d_sem, w_sem, s_sem,
):
    tokens = x.shape[0]
    nk = tokens // KB
    mats = (
        dict(d=dg, wh=wg, rs=rs_g, cs=cs_g),
        dict(d=du, wh=wu, rs=rs_u, cs=cs_u),
        dict(d=dd, wh=wd, rs=rs_d, cs=cs_d),
    )
    for mat, (m, n) in zip(mats, dims):
        mat["m"], mat["n"] = m, n

    def x_copy(k):
        return pltpu.make_async_copy(x.at[pl.ds(k * KB, KB), :], xs.at[k], x_sem.at[k])

    def h_copy(k):
        return pltpu.make_async_copy(h.at[pl.ds(k * KB, KB), :], hs.at[k % 3], h_sem.at[k % 3])

    tiles = [(q, j) for q in range(3) for j in range(mats[q]["n"] // NT)]

    def d_copy(i):
        q, j = tiles[i]
        return pltpu.make_async_copy(mats[q]["d"].at[:, pl.ds(j * NT, NT)], ring.at[i % RING], d_sem.at[i % RING])

    def w_copy(i, half):
        q, j = tiles[i]
        dst = held.at[pl.ds(block_rows(q, 1, 2 * j + half, dims), mats[q]["m"]), :]
        return pltpu.make_async_copy(mats[q]["wh"].at[:, pl.ds(j * NT + half * 128, 128)], dst, w_sem.at[i, half])

    small = [
        pltpu.make_async_copy(src, dst.at[q, 0, pl.ds(0, src.shape[0])], s_sem.at[i])
        for i, (src, dst, q) in enumerate(
            [(rg, ro, 0), (ru, ro, 1), (rd, ro, 2), (cg, co, 0), (cu, co, 1), (cd, co, 2)])
    ]
    x_copy(0).start()
    d_copy(0).start()
    for k in range(1, nk):
        x_copy(k).start()
    for i in range(1, RING - 1):
        d_copy(i).start()
    for c in small:
        c.start()

    def h_turn(k):
        for c in range(ht.shape[0] // 128):
            ht[pl.ds(c * 128, 128), pl.ds(k * KB, KB)] = hs[k % 3, :, pl.ds(c * 128, 128)].T

    def w_square(i):
        q, j = tiles[i]
        w = held[pl.ds(block_rows(q, 1, 2 * j, dims), 2 * mats[q]["m"]), :]
        s = jnp.sum((w * w).reshape(-1, 8, 128), axis=0)
        if j == 0:
            sw[q] = s
        else:
            sw[q] += s

    units = []
    for i, (q, j) in enumerate(tiles):
        if q < 2:
            units.append((i, q, j, (0, 256), 256))
        else:
            units.append((i, q, j, (0, 352), 352))
            units.append((i, q, j, (704, 1056), 352))
    n_units = len(units)

    before = [[] for _ in range(n_units)]
    beside = [[] for _ in range(n_units)]
    for k in range(nk):
        before[k].append(lambda k=k: h_copy(k).start())
        before[k + 2].append(lambda k=k: h_copy(k).wait())
        beside[k + 2].append(lambda k=k: h_turn(k))
    w_at = [3 + i for i in range(len(tiles))]
    for i in range(len(tiles)):
        u = min(w_at[i], n_units - 4)
        before[u].append(lambda i=i: [w_copy(i, half).start() for half in range(2)])
        before[u + 3].append(lambda i=i: [w_copy(i, half).wait() for half in range(2)])
        beside[u + 3].append(lambda i=i: w_square(i))
    def run(*accs):
        accs = [[accs[(z * 2 + par) * 3:(z * 2 + par) * 3 + 3] for par in range(2)] for z in range(2)]

        def rhs(u, k):
            return ring[units[u][0] % RING, pl.ds(k * KB, KB), :]

        def lhs(q, r0, rows, k):
            src = ht if q == 2 else xt
            return src[pl.ds(r0, rows), pl.ds(k * KB, KB)]

        def drain(u):
            i, q, j, starts, rows = units[u]
            mat = mats[q]
            cc = None
            for z in range(2):
                r0, left = starts[z], rows
                for p, size in enumerate(PIECES):
                    if not left:
                        break
                    g = pltpu.matmul_pop(accs[z][u % 2][p])
                    for half in range(2):
                        gr = block_rows(q, 0, 2 * j + half, dims) + r0
                        held[pl.ds(gr, size), :] = g[:, half * 128:half * 128 + 128]
                    s = g * g
                    lanes = s[:, :128] + s[:, 128:]
                    if j == 0:
                        mat["rs"][pl.ds(r0, size), :] = lanes
                    else:
                        mat["rs"][pl.ds(r0, size), :] += lanes
                    s = jnp.sum(s.reshape(-1, 8, NT), axis=0)
                    cc = s if cc is None else cc + s
                    r0, left = r0 + size, left - size
            if q == 2 and starts[0]:
                mat["cs"][:, pl.ds(j * NT, NT)] += cc
            else:
                mat["cs"][:, pl.ds(j * NT, NT)] = cc

        for z in range(2):
            for par in range(2):
                for p in range(3):
                    pltpu.matmul_pop(accs[z][par][p])

        d_copy(0).wait()
        for u in range(n_units):
            i, q, j, starts, rows = units[u]
            last = u == n_units - 1
            if u == 0:
                x_copy(0).wait()
            for f in before[u]:
                f()
            if not last and units[u + 1][0] != i:
                d_copy(units[u + 1][0]).wait()
            new = u == 0 or units[u - 1][0] != i
            if new and u and i + RING - 2 < len(tiles):
                d_copy(i + RING - 2).start()
            if u == 0:
                for z in range(2):
                    pltpu.matmul_push_rhs(rhs(0, 0), staging_register=0, mxu_index=z)
            for k in range(nk):
                if u == 0:
                    if k:
                        x_copy(k).wait()
                    for z in range(2):
                        xt[pl.ds(z * 256, 256), pl.ds(k * KB, KB)] = xs[k, :, pl.ds(z * 256, 256)].T
                for z in range(2):
                    r0, left = starts[z], rows
                    for p, size in enumerate(PIECES):
                        if not left:
                            break
                        pltpu.matmul_acc_lhs(accs[z][u % 2][p], lhs(q, r0, size, k),
                                             load_staged_rhs=(k % 2 if p == 0 else None))
                        r0, left = r0 + size, left - size
                    if k < nk - 1:
                        pltpu.matmul_push_rhs(rhs(u, k + 1), staging_register=(k + 1) % 2, mxu_index=z)
                    elif not last:
                        pltpu.matmul_push_rhs(rhs(u + 1, 0), staging_register=0, mxu_index=z)
                if k == 1 and u:
                    drain(u - 1)
                if k == 2:
                    for f in beside[u]:
                        f()
        drain(n_units - 1)

    spec = [pltpu.ACC(z)((size, NT), F32) for z in range(2) for par in range(2) for size in PIECES]
    pl.run_scoped(run, *spec)

    for c in small:
        c.wait()


def exchange_kernel(
    dims,
    held, rs_g, rs_u, rs_d, cs_g, cs_u, cs_d, sw, ro, co,
    b2, rel, clip,
    a_g, a_u, a_d, b_g, b_u, b_d, r_g, c_g, r_u, c_u, r_d, c_d,
    su, rsend, rrecv, csend, crecv, pay, got, r1s, r1r, c1s, c1r, p_s, p_r,
):
    col = lax.axis_index("col")
    row = lax.axis_index("row")
    row_peer = (row + 1 - 2 * (row % 2), (row + 2) % 4, 3 - row)
    mats = (
        dict(rs=rs_g, cs=cs_g, a=a_g, b=b_g, r=r_g, c=c_g),
        dict(rs=rs_u, cs=cs_u, a=a_u, b=b_u, r=r_u, c=c_u),
        dict(rs=rs_d, cs=cs_d, a=a_d, b=b_d, r=r_d, c=c_d),
    )
    for mat, (m, n) in zip(mats, dims):
        mat["m"], mat["n"] = m, n
        mat["mt"], mat["nt"] = mat["m"] * 4, mat["n"] * 2

    barrier = pltpu.get_barrier_semaphore()
    plane = [{"row": p, "col": cc} for cc in (col, 1 - col) for p in (row,) + row_peer][1:]
    for dev in plane:
        pl.semaphore_signal(barrier, inc=1, device_id=dev, device_id_type=MESH)
    pay[...] = jnp.zeros_like(pay)

    def first_sends(q):
        mat = mats[q]
        m, n = mat["m"], mat["n"]
        copies = [pltpu.make_async_remote_copy(
            rsend.at[q, :, pl.ds(0, m)], rrecv.at[q, :, pl.ds(0, m)], r1s.at[q], r1r.at[q],
            device_id={"col": 1 - col}, device_id_type=MESH)]
        for d in range(3):
            copies.append(pltpu.make_async_remote_copy(
                csend.at[q, :, pl.ds(0, n)], crecv.at[q, d, :, pl.ds(0, n)], c1s.at[q, d], c1r.at[q, d],
                device_id={"row": row_peer[d]}, device_id_type=MESH))
        return copies

    def first_reduce(q):
        mat = mats[q]
        csend[q, :, pl.ds(0, mat["n"])] = jnp.sum(mat["cs"][...], axis=0, keepdims=True)
        for b in range(mat["m"] // 128):
            t = mat["rs"][pl.ds(b * 128, 128), :].T
            rsend[q, :, pl.ds(b * 128, 128)] = jnp.sum(t, axis=0, keepdims=True)

    def new_stats(q):
        mat = mats[q]
        m, n = mat["m"], mat["n"]
        beta = b2[0, 0]
        rsum = rsend[q, :, pl.ds(0, m)] + rrecv[q, :, pl.ds(0, m)]
        r_new = beta * ro[q, :, pl.ds(0, m)] + (1.0 - beta) * (rsum * (1.0 / mat["nt"]) + EPS_SQ)
        mat["r"][...] = r_new
        csum = (csend[q, :, pl.ds(0, n)] + crecv[q, 0, :, pl.ds(0, n)]) + (
            crecv[q, 1, :, pl.ds(0, n)] + crecv[q, 2, :, pl.ds(0, n)])
        c_new = beta * co[q, :, pl.ds(0, n)] + (1.0 - beta) * (csum * (1.0 / mat["mt"]) + EPS_SQ)
        mat["c"][...] = c_new
        mat["b"][...] = lax.rsqrt(c_new)
        alpha = lax.rsqrt(r_new)
        rp = r_new[:, :128]
        for b in range(m // 128):
            blk = jnp.broadcast_to(alpha[:, b * 128:(b + 1) * 128], (128, 128))
            mat["a"][pl.ds(b * 128, 128), :] = blk.T
            if b:
                rp = rp + r_new[:, b * 128:(b + 1) * 128]
        pay[pl.ds(6 + q, 1), :] = rp

    def u_square(q):
        mat = mats[q]
        su[q] = jnp.zeros((8, 128), F32)

        @pl.loop(0, mat["n"] // 128)
        def _(c):
            cc = pl.ds(pl.multiple_of(c * 128, 128), 128)
            gr = pl.multiple_of(block_rows(q, 0, c, dims), 128)
            t = held[pl.ds(gr, mat["m"]), :] * mat["a"][...]
            s = jnp.sum((t * t).reshape(-1, 8, 128), axis=0)
            bb = mat["b"][:, cc]
            su[q] += s * (bb * bb)

    def pay_rows(q):
        pay[pl.ds(q, 1), :] = jnp.sum(su[q], axis=0, keepdims=True)
        pay[pl.ds(3 + q, 1), :] = jnp.sum(sw[q], axis=0, keepdims=True)

    for q in range(3):
        first_reduce(q)
    pl.semaphore_wait(barrier, len(plane))
    sends = [c for q in range(3) for c in first_sends(q)]
    for c in sends:
        c.start()
    for c in sends:
        c.wait()
    for q in range(3):
        new_stats(q)
    for q in range(3):
        u_square(q)
        pay_rows(q)
    sends = [pltpu.make_async_remote_copy(pay, got.at[i], p_s.at[i], p_r.at[i], device_id=dev, device_id_type=MESH)
             for i, dev in enumerate(plane)]
    for c in sends:
        c.start()
    for c in sends:
        c.wait()
    total = ((pay[...] + got[0]) + (got[1] + got[2])) + ((got[3] + got[4]) + (got[5] + got[6]))
    total = jnp.sum(total, axis=1, keepdims=True)
    for q, mat in enumerate(mats):
        size = float(mat["mt"] * mat["nt"])
        r_mean = total[6 + q:7 + q] * (0.5 / mat["mt"])
        u_rms = jnp.sqrt(r_mean * total[q:q + 1] / size)
        w_rms = jnp.sqrt(total[3 + q:4 + q] / size)
        step = rel[0, 0] * jnp.maximum(EPS_SCALE, w_rms)
        k = step * jnp.sqrt(r_mean) / jnp.maximum(1.0, u_rms / clip[0, 0])
        mat["b"][...] = mat["b"][...] * k


def write_kernel(
    dims,
    held, a_g, a_u, a_d, b_g, b_u, b_d, r_g, c_g, r_u, c_u, r_d, c_d,
    o_g, o_u, o_d, or_g, oc_g, or_u, oc_u, or_d, oc_d,
    wide, tall, o_sem, s_sem,
):
    small = [pltpu.make_async_copy(s.at[0], d, s_sem.at[i]) for i, (s, d) in enumerate(
        [(r_g, or_g), (c_g, oc_g), (r_u, or_u), (c_u, oc_u), (r_d, or_d), (c_d, oc_d)])]
    for c in small:
        c.start()
    slots = 4
    pending = {}
    step = 0
    for q, a, b, o, buf in ((2, a_d, b_d, o_d, tall), (1, a_u, b_u, o_u, wide), (0, a_g, b_g, o_g, wide)):
        rows = buf.shape[1]
        for t in range(dims[q][0] // rows):
            slot = step % slots
            if slot in pending:
                pending.pop(slot).wait()
            rr = pl.ds(t * rows, rows)
            scale = a[rr, :]
            for c in range(dims[q][1] // 128):
                cc = pl.ds(c * 128, 128)
                g, w = (held[pl.ds(block_rows(q, z, c, dims) + t * rows, rows), :] for z in range(2))
                buf[slot, :, cc] = w - (g * scale) * b[:, cc]
            cp = pltpu.make_async_copy(buf.at[slot], o.at[rr, :], o_sem.at[slot])
            cp.start()
            pending[slot] = cp
            step += 1
    for cp in pending.values():
        cp.wait()
    for c in small:
        c.wait()


def solution(mesh):
    def local_program(x_in, h_act, d_gate, d_up, d_out, w_gate, w_up, w_down, r_gate, c_gate, r_up, c_up, r_down, c_down, beta_two, rel_step, clip_thr):
        (mg, ng), (md, nd) = w_gate.shape, w_down.shape
        tokens = x_in.shape[0]
        nk = tokens // KB
        big = [x_in, h_act, d_gate, d_up, d_out, w_gate, w_up, w_down, r_gate, c_gate, r_up, c_up, r_down, c_down]
        one = [v.reshape(1, 1) for v in (beta_two, rel_step, clip_thr)]
        big = [pltpu.with_memory_space_constraint(v, HB) for v in big]
        dims = [(mg, ng), (mg, ng), (md, nd)]
        mm, nn = max(mg, md), max(ng, nd)
        dma = pltpu.SemaphoreType.DMA

        def call(kernel, outs, args, in_spaces, out_space, scratch, mib, **params):
            return pl.pallas_call(
                functools.partial(kernel, dims),
                out_shape=outs,
                in_specs=[pl.BlockSpec(memory_space=v) for v in in_spaces],
                out_specs=tuple(pl.BlockSpec(memory_space=out_space) for _ in outs),
                scratch_shapes=scratch,
                compiler_params=pltpu.CompilerParams(vmem_limit_bytes=mib * 2**20, **params),
                name=kernel.__name__,
            )(*args)

        def vm(shapes):
            return tuple(VM(s, F32) for s in shapes)

        lanes = [(m, 128) for m, _ in dims]
        first = call(
            dot_kernel,
            vm([(2 * sum(m * n for m, n in dims) // 128, 128)] + lanes + [(8, n) for _, n in dims] + [(3, 8, 128), (3, 1, mm), (3, 1, nn)]),
            big, [HB] * len(big), VM,
            [
                VM((nk, KB, mg), BF16), VM((3, KB, md), BF16), VM((mg, tokens), BF16), VM((md, tokens), BF16),
                VM((RING, tokens, NT), BF16),
                dma((nk,)), dma((3,)), dma((RING,)), dma((2 * ng // NT + nd // NT, 2)), dma((6,)),
            ], 22)
        held, rest = first[:1], first[1:]
        stats = [s for m, n in dims for s in ((1, m), (1, n))]
        second = call(
            exchange_kernel,
            vm(lanes + [(1, n) for _, n in dims] + stats),
            held + rest + tuple(one), [VM] * len(first) + [pltpu.SMEM] * 3, VM,
            [
                VM((3, 8, 128), F32),
                VM((3, 1, mm), F32), VM((3, 1, mm), F32), VM((3, 1, nn), F32), VM((3, 3, 1, nn), F32),
                VM((16, 128), F32), VM((7, 16, 128), F32),
                dma((3,)), dma((3,)), dma((3, 3)), dma((3, 3)), dma((7,)), dma((7,)),
            ], 8, collective_id=0, has_side_effects=True)
        outs = call(
            write_kernel,
            tuple(jax.ShapeDtypeStruct(s, F32) for s in dims + [(k,) for mn in dims for k in mn]),
            held + second, [VM] * (1 + len(second)), HB,
            [VM((4, mg // 8, ng), F32), VM((4, md // 8, nd), F32), dma((4,)), dma((6,))], 8)
        return tuple(outs)

    act_spec = P(None, "row")
    cot_spec = P(None, "col")
    w_spec = P("row", "col")
    r_spec = P("row")
    c_spec = P("col")
    s_spec = P()
    return jax.shard_map(local_program, mesh=mesh, in_specs=(act_spec, act_spec, cot_spec, cot_spec, cot_spec, w_spec, w_spec, w_spec, r_spec, c_spec, r_spec, c_spec, r_spec, c_spec, s_spec, s_spec, s_spec), out_specs=(w_spec, w_spec, w_spec, r_spec, c_spec, r_spec, c_spec, r_spec, c_spec), check_vma=False)
```

time: 115 us -> 70.7 us (0.61)
  Pallas kernels: 0 us -> 45.5 us
  other arithmetic: 41.9 us -> 0 us
  blocking collectives: 33.9 us -> 0 us
  matrix products: 28.4 us -> 0 us
  local copies, waits for them, and re-layouts: 0.97 us -> 22.2 us
  between operations: 9.06 us -> 2.77 us
    pallas_call x0 -> x3, Pallas kernels: none -> 45.5 us  [call(): pl.pallas_call(functools.partial(kernel, dims), out_shape=outs, in_specs=...]
    psum x3 -> x0, blocking collectives: 33.9 us -> none  [the longest x1 12.6 us: block_step(): lax.psum(jnp.sum(u_blk * u_blk), ('row', 'col')) / (m_total * n_total)]
    dot_general x3 -> x0, matrix products: 28.4 us -> none  [block_step(): lax.dot_general(act_in, cot_out, CONTRACT_TOKENS, preferred_element_type=...]
    reduce_sum x7 -> x0, other arithmetic: 24.1 us -> none  [the longest x3 12.4 us: block_step(): jnp.sum(u_blk * u_blk)]
    unnamed x50 -> x4, local copies, waits for them, and re-layouts: 0.97 us -> 22.2 us
    sub x3 -> x0, other arithmetic: 17.7 us -> none  [block_step(): return (w_blk - step_size * u_hat, r_new, c_new)]
where the time goes in v1:
time: 70.7 us; the launch traced here: 70.5 us
  Pallas kernels  45.5 us (64%)
  local copies, waits for them, and re-layouts  22.2 us (31%)
  between operations  2.77 us (4%)
    pallas_call x3, Pallas kernels, call(): pl.pallas_call(functools.partial(kernel, dims), out_shape=outs, in_specs=...  45.5 us
    unnamed x4, local copies, waits for them, and re-layouts  22.2 us

profile of v1, /device:TPU:0, one launch (start us, length us, event | category | flops | bytes accessed | tf_op | source)
XLA Modules:
  0.0 70.5 jit_solution(917606399216449328)
XLA Ops:
  2.6 23.4 %dot_kernel.1 = (f32[67584,128]{1,0:T(8,128)S(1)}, f32[512,128]{1,0:T(8,128)S(1)}, f32[512,128]{1,0:T(8,128)S(1)}, f32[1408,128]{1,0:T(8,128)S(1)}, f32[8,2816]{...) custom-call(bf16[2048,512]{1,0:T(8,128)(2,1)} %x.1, ...), custom_call_target="tpu_custom_call" | custom-call | tf_op jit(solution)/shard_map/dot_kernel/pallas_call | solution.py:362
  26.0 0.0 copy-start
  26.0 11.4 %copy-done = f32[67584,128]{1,0:T(8,128)} copy-done((f32[67584,128]{1,0:T(8,128)}, f32[67584,128]{1,0:T(8,128)S(1)}, u32[]{:S(2)}) %copy-start) | copy-done | bytes 34603032
  37.4 0.0 copy-start.1
  37.4 10.8 %copy-done.1 = f32[67584,128]{1,0:T(8,128)S(1)} copy-done((f32[67584,128]{1,0:T(8,128)S(1)}, f32[67584,128]{1,0:T(8,128)}, u32[]{:S(2)}) %copy-start.1) | copy-done | bytes 34603032
  48.3 15.6 %exchange_kernel.1 = (f32[512,128]{1,0:T(8,128)S(1)}, f32[512,128]{1,0:T(8,128)S(1)}, f32[1408,128]{1,0:T(8,128)S(1)}, f32[1,2816]{1,0:T(1,128)S(1)}, f32[1,2816...) custom-call(f32[67584,128]{1,0:T(8,128)S(1)} %copy-done.1, ...), custom_call_target="tpu_custom_call" | custom-call | tf_op jit(solution)/shard_map/exchange_kernel/pallas_call | solution.py:362
  63.8 6.5 %write_kernel.1 = (f32[512,2816]{1,0:T(8,128)}, f32[512,2816]{1,0:T(8,128)}, f32[1408,1024]{1,0:T(8,128)}, f32[512]{0:T(512)}, f32[2816]{0:T(1024)}, /*index=5*/...) custom-call(f32[67584,128]{1,0:T(8,128)S(1)} %copy-done.1, f32[512,128]{1,0:T(8,128)S(1)} %get-tuple-element.41.a_g, ...), custom_call_target="tpu_custom_call" | custom-call | tf_op jit(solution)/shard_map/write_kernel/pallas_call | solution.py:362
Async XLA Ops:
  26.0 11.4 %copy-start = (f32[67584,128]{1,0:T(8,128)}, f32[67584,128]{1,0:T(8,128)S(1)}, u32[]{:S(2)}) copy-start(f32[67584,128]{1,0:T(8,128)S(1)} %get-tuple-element.31.held) | copy-start | bytes 103809024
  37.4 10.8 %copy-start.1 = (f32[67584,128]{1,0:T(8,128)S(1)}, f32[67584,128]{1,0:T(8,128)}, u32[]{:S(2)}) copy-start(f32[67584,128]{1,0:T(8,128)} %copy-done) | copy-start | bytes 103809024

commit v2 on v1

--- a/solution.py
+++ b/solution.py
@@ -16,7 +16,7 @@
 HB = pltpu.HBM
 KB = 256
 NT = 256
-RING = 8
+RING = 4
 PIECES = (176, 80, 96)
 
 
@@ -381,7 +381,7 @@
                 VM((nk, KB, mg), BF16), VM((3, KB, md), BF16), VM((mg, tokens), BF16), VM((md, tokens), BF16),
                 VM((RING, tokens, NT), BF16),
                 dma((nk,)), dma((3,)), dma((RING,)), dma((2 * ng // NT + nd // NT, 2)), dma((6,)),
-            ], 22)
+            ], 18)
         held, rest = first[:1], first[1:]
         stats = [s for m, n in dims for s in ((1, m), (1, n))]
         second = call(
@@ -393,12 +393,12 @@
                 VM((3, 1, mm), F32), VM((3, 1, mm), F32), VM((3, 1, nn), F32), VM((3, 3, 1, nn), F32),
                 VM((16, 128), F32), VM((7, 16, 128), F32),
                 dma((3,)), dma((3,)), dma((3, 3)), dma((3, 3)), dma((7,)), dma((7,)),
-            ], 8, collective_id=0, has_side_effects=True)
+            ], 18, collective_id=0, has_side_effects=True)
         outs = call(
             write_kernel,
             tuple(jax.ShapeDtypeStruct(s, F32) for s in dims + [(k,) for mn in dims for k in mn]),
             held + second, [VM] * (1 + len(second)), HB,
-            [VM((4, mg // 8, ng), F32), VM((4, md // 8, nd), F32), dma((4,)), dma((6,))], 8)
+            [VM((4, mg // 8, ng), F32), VM((4, md // 8, nd), F32), dma((4,)), dma((6,))], 18)
         return tuple(outs)
 
     act_spec = P(None, "row")

time: 70.7 us -> 62.3 us (0.88)
  local copies, waits for them, and re-layouts: 22.2 us -> 0 us
  Pallas kernels: 45.5 us -> 58.9 us
    unnamed x4 -> x0, local copies, waits for them, and re-layouts: 22.2 us -> none
    pallas_call x3, Pallas kernels: 45.5 us -> 58.9 us  [call(): pl.pallas_call(functools.partial(kernel, dims), out_shape=outs, in_specs=...]
where the time goes in v2:
time: 62.3 us; the launch traced here: 61.6 us
  Pallas kernels  58.9 us (95%)
  between operations  2.76 us (4%)
    pallas_call x3, Pallas kernels, call(): pl.pallas_call(functools.partial(kernel, dims), out_shape=outs, in_specs=...  58.9 us

profile of v2, /device:TPU:0, one launch (start us, length us, event | category | flops | bytes accessed | tf_op | source)
XLA Modules:
  0.0 61.6 jit_solution(7400606075403416674)
XLA Ops:
  2.6 36.8 %dot_kernel.1 = (f32[67584,128]{1,0:T(8,128)S(1)}, f32[512,128]{1,0:T(8,128)S(1)}, f32[512,128]{1,0:T(8,128)S(1)}, f32[1408,128]{1,0:T(8,128)S(1)}, f32[8,2816]{...) custom-call(bf16[2048,512]{1,0:T(8,128)(2,1)} %x.1, ...), custom_call_target="tpu_custom_call" | custom-call | tf_op jit(solution)/shard_map/dot_kernel/pallas_call | solution.py:362
  39.4 15.6 %exchange_kernel.1 = (f32[512,128]{1,0:T(8,128)S(1)}, f32[512,128]{1,0:T(8,128)S(1)}, f32[1408,128]{1,0:T(8,128)S(1)}, f32[1,2816]{1,0:T(1,128)S(1)}, f32[1,2816...) custom-call(f32[67584,128]{1,0:T(8,128)S(1)} %get-tuple-element.31.h, ...), custom_call_target="tpu_custom_call" | custom-call | tf_op jit(solution)/shard_map/exchange_kernel/pallas_call | solution.py:362
  55.0 6.5 %write_kernel.1 = (f32[512,2816]{1,0:T(8,128)}, f32[512,2816]{1,0:T(8,128)}, f32[1408,1024]{1,0:T(8,128)}, f32[512]{0:T(512)}, f32[2816]{0:T(1024)}, /*index=5*/...) custom-call(f32[67584,128]{1,0:T(8,128)S(1)} %get-tuple-element.31.held, f32[512,128]{1,0:T(8,128)S(1)} %get-tuple-element.41.a_g, ...), custom_call_target="tpu_custom_call" | custom-call | tf_op jit(solution)/shard_map/write_kernel/pallas_call | solution.py:362

commit v3 on v2

--- a/solution.py
+++ b/solution.py
@@ -16,7 +16,7 @@
 HB = pltpu.HBM
 KB = 256
 NT = 256
-RING = 4
+RING = 12
 PIECES = (176, 80, 96)
 
 
@@ -321,7 +321,7 @@
         [(r_g, or_g), (c_g, oc_g), (r_u, or_u), (c_u, oc_u), (r_d, or_d), (c_d, oc_d)])]
     for c in small:
         c.start()
-    slots = 4
+    slots = 8
     pending = {}
     step = 0
     for q, a, b, o, buf in ((2, a_d, b_d, o_d, tall), (1, a_u, b_u, o_u, wide), (0, a_g, b_g, o_g, wide)):
@@ -381,24 +381,24 @@
                 VM((nk, KB, mg), BF16), VM((3, KB, md), BF16), VM((mg, tokens), BF16), VM((md, tokens), BF16),
                 VM((RING, tokens, NT), BF16),
                 dma((nk,)), dma((3,)), dma((RING,)), dma((2 * ng // NT + nd // NT, 2)), dma((6,)),
-            ], 18)
+            ], 26)
         held, rest = first[:1], first[1:]
         stats = [s for m, n in dims for s in ((1, m), (1, n))]
         second = call(
             exchange_kernel,
             vm(lanes + [(1, n) for _, n in dims] + stats),
-            held + rest + tuple(one), [VM] * len(first) + [pltpu.SMEM] * 3, VM,
+            tuple(pltpu.with_memory_space_constraint(v, VM) for v in held + rest) + tuple(one), [VM] * len(first) + [pltpu.SMEM] * 3, VM,
             [
                 VM((3, 8, 128), F32),
                 VM((3, 1, mm), F32), VM((3, 1, mm), F32), VM((3, 1, nn), F32), VM((3, 3, 1, nn), F32),
                 VM((16, 128), F32), VM((7, 16, 128), F32),
                 dma((3,)), dma((3,)), dma((3, 3)), dma((3, 3)), dma((7,)), dma((7,)),
-            ], 18, collective_id=0, has_side_effects=True)
+            ], 26, collective_id=0, has_side_effects=True)
         outs = call(
             write_kernel,
             tuple(jax.ShapeDtypeStruct(s, F32) for s in dims + [(k,) for mn in dims for k in mn]),
-            held + second, [VM] * (1 + len(second)), HB,
-            [VM((4, mg // 8, ng), F32), VM((4, md // 8, nd), F32), dma((4,)), dma((6,))], 18)
+            tuple(pltpu.with_memory_space_constraint(v, VM) for v in held + second), [VM] * (1 + len(second)), HB,
+            [VM((8, mg // 8, ng), F32), VM((8, md // 8, nd), F32), dma((8,)), dma((6,))], 26)
         return tuple(outs)
 
     act_spec = P(None, "row")

time: 62.3 us -> 49.5 us (0.79)
  Pallas kernels: 58.9 us -> 46.5 us
    pallas_call x3, Pallas kernels: 58.9 us -> 46.5 us  [call(): pl.pallas_call(functools.partial(kernel, dims), out_shape=outs, in_specs=...]
where the time goes in v3:
time: 49.5 us; the launch traced here: 49.3 us
  Pallas kernels  46.5 us (94%)
  between operations  2.76 us (6%)
    pallas_call x3, Pallas kernels, call(): pl.pallas_call(functools.partial(kernel, dims), out_shape=outs, in_specs=...  46.5 us

profile of v3, /device:TPU:0, one launch (start us, length us, event | category | flops | bytes accessed | tf_op | source)
XLA Modules:
  0.0 49.3 jit_solution(1059332899253209207)
XLA Ops:
  2.6 24.7 %dot_kernel.1 = (f32[67584,128]{1,0:T(8,128)S(1)}, f32[512,128]{1,0:T(8,128)S(1)}, f32[512,128]{1,0:T(8,128)S(1)}, f32[1408,128]{1,0:T(8,128)S(1)}, f32[8,2816]{...) custom-call(bf16[2048,512]{1,0:T(8,128)(2,1)} %x.1, ...), custom_call_target="tpu_custom_call" | custom-call | tf_op jit(solution)/shard_map/dot_kernel/pallas_call | solution.py:362
  27.3 15.6 %exchange_kernel.1 = (f32[512,128]{1,0:T(8,128)S(1)}, f32[512,128]{1,0:T(8,128)S(1)}, f32[1408,128]{1,0:T(8,128)S(1)}, f32[1,2816]{1,0:T(1,128)S(1)}, f32[1,2816...) custom-call(f32[67584,128]{1,0:T(8,128)S(1)} %get-tuple-element.31.h, ...), custom_call_target="tpu_custom_call" | custom-call | tf_op jit(solution)/shard_map/exchange_kernel/pallas_call | solution.py:362
  42.9 6.2 %write_kernel.1 = (f32[512,2816]{1,0:T(8,128)}, f32[512,2816]{1,0:T(8,128)}, f32[1408,1024]{1,0:T(8,128)}, f32[512]{0:T(512)}, f32[2816]{0:T(1024)}, /*index=5*/...) custom-call(f32[67584,128]{1,0:T(8,128)S(1)} %get-tuple-element.31.held, f32[512,128]{1,0:T(8,128)S(1)} %get-tuple-element.41.a_g, ...), custom_call_target="tpu_custom_call" | custom-call | tf_op jit(solution)/shard_map/write_kernel/pallas_call | solution.py:362

commit v4 on v3

v4 whole, which is shorter than its diff:
```python
import functools

import jax
import jax.numpy as jnp
from jax import lax
from jax.experimental import pallas as pl
from jax.experimental.pallas import tpu as pltpu
from jax.sharding import PartitionSpec as P

EPS_SQ = 1e-30
EPS_SCALE = 1e-3
F32 = jnp.float32
BF16 = jnp.bfloat16
MESH = pl.DeviceIdType.MESH
VM = pltpu.VMEM
HB = pltpu.HBM
KB = 256
NT = 256
RING = 11
PIECES = (128, 128)
GRANT = 18
CHUNKS = 4


def fold(v):
    slabs = v.reshape(-1, 8, v.shape[1])
    n = slabs.shape[0] // 4 * 4
    s = jnp.sum(slabs[:n].reshape(-1, 4, 8, v.shape[1]), axis=0)
    s = (s[0] + s[1]) + (s[2] + s[3])
    for i in range(n, slabs.shape[0]):
        s = s + slabs[i]
    return s


def dot_kernel(
    dims,
    x, h, dg, du, dd, wg, rg, cg, ru, cu, rd, cd,
    held, ht, dt, rs_g, rs_u, cs_g, cs_u, sw, ro, co,
    xs, hs, xt, ring, x_sem, h_sem, d_sem, first_sem, t_sem, w_sem, s_sem,
):
    m, n = dims[0]
    nk = x.shape[0] // KB
    up = n // NT
    cots, rss, css = (dg, du), (rs_g, rs_u), (cs_g, cs_u)
    n_units = 2 * up

    def x_copy(k):
        return pltpu.make_async_copy(x.at[pl.ds(k * KB, KB), :], xs.at[k], x_sem.at[k])

    def h_copy(k):
        return pltpu.make_async_copy(h.at[pl.ds(k * KB, KB), :], hs.at[k % 3], h_sem.at[k % 3])

    def d_copy(u):
        q, j = divmod(u, up)
        return pltpu.make_async_copy(cots[q].at[:, pl.ds(j * NT, NT)], ring.at[u % RING], d_sem.at[u % RING])

    def first_copy(k):
        return pltpu.make_async_copy(dg.at[pl.ds(k * KB, KB), pl.ds(0, NT)], ring.at[0, pl.ds(k * KB, KB), :], first_sem.at[k])

    def t_copy(j):
        return pltpu.make_async_copy(dd.at[:, pl.ds(j * NT, NT)], dt.at[j], t_sem.at[j])

    def w_copy(c):
        return pltpu.make_async_copy(wg.at[:, pl.ds(c * 128, 128)], held.at[pl.ds(2 * m * (n // 128) + c * m, m), :], w_sem.at[c])

    small = [
        pltpu.make_async_copy(src, dst.at[q, 0, pl.ds(0, src.shape[0])], s_sem.at[i])
        for i, (src, dst, q) in enumerate(
            [(rg, ro, 0), (ru, ro, 1), (rd, ro, 2), (cg, co, 0), (cu, co, 1), (cd, co, 2)])
    ]
    for k in range(nk):
        x_copy(k).start()
        first_copy(k).start()

    def h_turn(k):
        for c in range(ht.shape[0] // 128):
            ht[pl.ds(c * 128, 128), pl.ds(k * KB, KB)] = hs[k % 3, :, pl.ds(c * 128, 128)].T

    def w_square(c):
        w = held[pl.ds(2 * m * (n // 128) + c * m, m), :]
        s = fold(w * w)
        if c == 0:
            sw[...] = s
        else:
            sw[...] += s

    before = [[] for _ in range(n_units)]
    beside = [[] for _ in range(n_units)]
    for k in range(nk):
        before[k + 1].append(lambda k=k: h_copy(k).start())
        before[k + 3].append(lambda k=k: h_copy(k).wait())
        beside[k + 3].append(lambda k=k: h_turn(k))
    for j in range(dt.shape[0]):
        before[10 + 2 * j].append(lambda j=j: t_copy(j).start())
        before[min(16 + 2 * j, n_units - 1)].append(lambda j=j: t_copy(j).wait())
    for c in range(n // 128):
        u = 9 + c // 3
        before[u].append(lambda c=c: w_copy(c).start())
        before[u + 4].append(lambda c=c: w_copy(c).wait())
        beside[u + 4].append(lambda c=c: w_square(c))
    before[8].append(lambda: [c.start() for c in small])
    before[20].append(lambda: [c.wait() for c in small])

    def run(*accs):
        def acc(z, par, p):
            return accs[(z * 2 + par) * 2 + p]

        def rhs(u, k):
            return ring[u % RING, pl.ds(k * KB, KB), :]

        def drain(u):
            q, j = divmod(u, up)
            cc = None
            for z in range(2):
                for p, size in enumerate(PIECES):
                    r0 = z * sum(PIECES) + sum(PIECES[:p])
                    g = pltpu.matmul_pop(acc(z, u % 2, p))
                    for half in range(2):
                        held[pl.ds((q * (n // 128) + 2 * j + half) * m + r0, size), :] = g[:, half * 128:half * 128 + 128]
                    s = g * g
                    lanes = s[:, :128] + s[:, 128:]
                    if j == 0:
                        rss[q][pl.ds(r0, size), :] = lanes
                    else:
                        rss[q][pl.ds(r0, size), :] += lanes
                    s = fold(s)
                    cc = s if cc is None else cc + s
            css[q][:, pl.ds(j * NT, NT)] = cc

        for z in range(2):
            for par in range(2):
                for p in range(2):
                    pltpu.matmul_pop(acc(z, par, p))

        for u in range(n_units):
            last = u == n_units - 1
            for f in before[u]:
                f()
            if u:
                if not last:
                    d_copy(u + 1).wait()
                if u + RING - 2 < n_units:
                    d_copy(u + RING - 2).start()
            for k in range(nk):
                if u == 0:
                    x_copy(k).wait()
                    first_copy(k).wait()
                    for z in range(2):
                        xt[pl.ds(z * 256, 256), pl.ds(k * KB, KB)] = xs[k, :, pl.ds(z * 256, 256)].T
                        pltpu.matmul_push_rhs(rhs(0, k), staging_register=k % 2, mxu_index=z)
                    if k == 0:
                        for i in range(1, 4):
                            d_copy(i).start()
                    elif k + 3 <= RING - 2:
                        d_copy(k + 3).start()
                    if k == nk - 1:
                        for i in range(nk + 3, RING - 1):
                            d_copy(i).start()
                        d_copy(1).wait()
                for z in range(2):
                    for p, size in enumerate(PIECES):
                        r0 = z * sum(PIECES) + sum(PIECES[:p])
                        pltpu.matmul_acc_lhs(acc(z, u % 2, p), xt[pl.ds(r0, size), pl.ds(k * KB, KB)],
                                             load_staged_rhs=(k % 2 if p == 0 else None))
                    if k < nk - 1:
                        if u:
                            pltpu.matmul_push_rhs(rhs(u, k + 1), staging_register=(k + 1) % 2, mxu_index=z)
                    elif not last:
                        pltpu.matmul_push_rhs(rhs(u + 1, 0), staging_register=0, mxu_index=z)
                if k == 1 and u:
                    drain(u - 1)
                if k == 2:
                    for f in beside[u]:
                        f()
        drain(n_units - 1)

    pl.run_scoped(run, *[pltpu.ACC(z)((size, NT), F32) for z in range(2) for par in range(2) for size in PIECES])


def exchange_kernel(
    dims,
    held, ht, dt, rs_g, rs_u, cs_g, cs_u, sw_g, ro, co,
    wu, wd,
    b2, rel, clip,
    late, a_g, a_u, a_d, b_g, b_u, b_d, r_g, c_g, r_u, c_u, r_d, c_d,
    rs_d, cs_d, su, sw, rsend, rrecv, csend, crecv, pay, got, w_sem, r1s, r1r, c1s, c1r, p_s, p_r,
):
    col = lax.axis_index("col")
    row = lax.axis_index("row")
    row_peer = (row + 1 - 2 * (row % 2), (row + 2) % 4, 3 - row)
    mats = (
        dict(rs=rs_g, cs=cs_g, a=a_g, b=b_g, r=r_g, c=c_g),
        dict(rs=rs_u, cs=cs_u, a=a_u, b=b_u, r=r_u, c=c_u),
        dict(rs=rs_d, cs=cs_d, a=a_d, b=b_d, r=r_d, c=c_d),
    )
    for mat, (m, n) in zip(mats, dims):
        mat["m"], mat["n"] = m, n
        mat["mt"], mat["nt"] = m * 4, n * 2
    (mg, ng), (md, nd) = dims[0], dims[2]
    size = mg * ng // 128

    barrier = pltpu.get_barrier_semaphore()
    plane = [{"row": p, "col": cc} for cc in (col, 1 - col) for p in (row,) + row_peer][1:]
    for dev in plane:
        pl.semaphore_signal(barrier, inc=1, device_id=dev, device_id_type=MESH)

    def w_copy(i):
        q, c = (1, i) if i < ng // 128 else (2, i - ng // 128)
        m = dims[q][0]
        return pltpu.make_async_copy((wu, wd)[q - 1].at[:, pl.ds(c * 128, 128)], late.at[pl.ds(q * size + c * m, m), :], w_sem.at[i])

    blocks = ng // 128 + nd // 128
    for i in range(blocks):
        w_copy(i).start()
    pay[...] = jnp.zeros_like(pay)
    sw[0] = sw_g[...]

    def w_square(i):
        q, c = (1, i) if i < ng // 128 else (2, i - ng // 128)
        m = dims[q][0]
        w = late[pl.ds(q * size + c * m, m), :]
        s = fold(w * w)
        if c == 0:
            sw[q] = s
        else:
            sw[q] += s

    def first_sends(q):
        mat = mats[q]
        m, n = mat["m"], mat["n"]
        copies = [pltpu.make_async_remote_copy(
            rsend.at[q, :, pl.ds(0, m)], rrecv.at[q, :, pl.ds(0, m)], r1s.at[q], r1r.at[q],
            device_id={"col": 1 - col}, device_id_type=MESH)]
        for d in range(3):
            copies.append(pltpu.make_async_remote_copy(
                csend.at[q, :, pl.ds(0, n)], crecv.at[q, d, :, pl.ds(0, n)], c1s.at[q, d], c1r.at[q, d],
                device_id={"row": row_peer[d]}, device_id_type=MESH))
        return copies

    def first_reduce(q):
        mat = mats[q]
        csend[q, :, pl.ds(0, mat["n"])] = jnp.sum(mat["cs"][...], axis=0, keepdims=True)
        for b in range(mat["m"] // 128):
            t = mat["rs"][pl.ds(b * 128, 128), :].T
            rsend[q, :, pl.ds(b * 128, 128)] = jnp.sum(t, axis=0, keepdims=True)

    def new_stats(q):
        mat = mats[q]
        m, n = mat["m"], mat["n"]
        beta = b2[0, 0]
        rsum = rsend[q, :, pl.ds(0, m)] + rrecv[q, :, pl.ds(0, m)]
        r_new = beta * ro[q, :, pl.ds(0, m)] + (1.0 - beta) * (rsum * (1.0 / mat["nt"]) + EPS_SQ)
        mat["r"][...] = r_new
        csum = (csend[q, :, pl.ds(0, n)] + crecv[q, 0, :, pl.ds(0, n)]) + (
            crecv[q, 1, :, pl.ds(0, n)] + crecv[q, 2, :, pl.ds(0, n)])
        c_new = beta * co[q, :, pl.ds(0, n)] + (1.0 - beta) * (csum * (1.0 / mat["mt"]) + EPS_SQ)
        mat["c"][...] = c_new
        mat["b"][...] = lax.rsqrt(c_new)
        alpha = lax.rsqrt(r_new)
        rp = r_new[:, :128]
        for b in range(m // 128):
            blk = jnp.broadcast_to(alpha[:, b * 128:(b + 1) * 128], (128, 128))
            mat["a"][pl.ds(b * 128, 128), :] = blk.T
            if b:
                rp = rp + r_new[:, b * 128:(b + 1) * 128]
        pay[pl.ds(6 + q, 1), :] = rp

    def u_square(q, c):
        mat = mats[q]
        m = mat["m"]
        g = late[pl.ds(c * m, m), :] if q == 2 else held[pl.ds(q * size + c * m, m), :]
        t = g * mat["a"][...]
        bb = mat["b"][:, c * 128:(c + 1) * 128]
        s = fold(t * t) * (bb * bb)
        if c == 0:
            su[q] = s
        else:
            su[q] += s

    def pay_rows(q):
        pay[pl.ds(q, 1), :] = jnp.sum(su[q], axis=0, keepdims=True)
        pay[pl.ds(3 + q, 1), :] = jnp.sum(sw[q], axis=0, keepdims=True)

    rows = md // CHUNKS
    steps = nd // NT * CHUNKS

    def product(i):
        j, c = divmod(i, CHUNKS)
        rr = pl.ds(c * rows, rows)
        g = jnp.dot(ht[rr, :], dt[j], preferred_element_type=F32)
        for half in range(2):
            late[pl.ds((2 * j + half) * md + c * rows, rows), :] = g[:, half * 128:half * 128 + 128]
        s = g * g
        lanes = s[:, :128] + s[:, 128:]
        if j == 0:
            rs_d[rr, :] = lanes
        else:
            rs_d[rr, :] += lanes
        cc = pl.ds(j * NT, NT)
        if c == 0:
            cs_d[:, cc] = fold(s)
        else:
            cs_d[:, cc] += fold(s)

    sends = [c for q in range(2) for c in first_sends(q)]
    tasks = [[] for _ in range(steps)]
    tasks[0] = [lambda: first_reduce(0), lambda: first_reduce(1)]
    for i in range(blocks):
        tasks[3 + i * (steps - 3) // blocks].append(lambda i=i: w_square(i))
    todo = [(q, c) for q in range(2) for c in range(ng // 128)]
    at = 10
    for t, (q, c) in enumerate(todo):
        tasks[at + t * (steps - at) // len(todo)].append(lambda q=q, c=c: u_square(q, c))
    seen = 0
    for i in range(steps):
        if i == 4:
            pl.semaphore_wait(barrier, len(plane))
            for c in sends:
                c.start()
        if i == at:
            for c in sends:
                c.wait()
            new_stats(0)
            new_stats(1)
        if i >= 3:
            while seen < blocks and 3 + seen * (steps - 3) // blocks == i:
                w_copy(seen).wait()
                seen += 1
        product(i)
        for f in tasks[i]:
            f()
    pay_rows(0)
    pay_rows(1)

    first_reduce(2)
    sends = first_sends(2)
    for c in sends:
        c.start()
    for c in sends:
        c.wait()
    new_stats(2)
    for c in range(nd // 128):
        u_square(2, c)
    pay_rows(2)
    sends = [pltpu.make_async_remote_copy(pay, got.at[i], p_s.at[i], p_r.at[i], device_id=dev, device_id_type=MESH)
             for i, dev in enumerate(plane)]
    for c in sends:
        c.start()
    for c in sends:
        c.wait()
    total = ((pay[...] + got[0]) + (got[1] + got[2])) + ((got[3] + got[4]) + (got[5] + got[6]))
    total = jnp.sum(total, axis=1, keepdims=True)
    for q, mat in enumerate(mats):
        size = float(mat["mt"] * mat["nt"])
        r_mean = total[6 + q:7 + q] * (0.5 / mat["mt"])
        u_rms = jnp.sqrt(r_mean * total[q:q + 1] / size)
        w_rms = jnp.sqrt(total[3 + q:4 + q] / size)
        step = rel[0, 0] * jnp.maximum(EPS_SCALE, w_rms)
        k = step * jnp.sqrt(r_mean) / jnp.maximum(1.0, u_rms / clip[0, 0])
        mat["b"][...] = mat["b"][...] * k


def write_kernel(
    dims,
    held, ht, dt, rs_g, rs_u, cs_g, cs_u, sw_g, ro, co,
    late, a_g, a_u, a_d, b_g, b_u, b_d, r_g, c_g, r_u, c_u, r_d, c_d,
    o_g, o_u, o_d, or_g, oc_g, or_u, oc_u, or_d, oc_d,
    wide, tall, o_sem, s_sem,
):
    small = [pltpu.make_async_copy(s.at[0], d, s_sem.at[i]) for i, (s, d) in enumerate(
        [(r_g, or_g), (c_g, oc_g), (r_u, or_u), (c_u, oc_u), (r_d, or_d), (c_d, oc_d)])]
    for c in small:
        c.start()
    slots = 8
    size = dims[0][0] * dims[0][1] // 128
    where = (((held, 0), (held, 2)), ((held, 1), (late, 1)), ((late, 0), (late, 2)))
    pending = {}
    step = 0
    for q, a, b, o, buf in ((2, a_d, b_d, o_d, tall), (1, a_u, b_u, o_u, wide), (0, a_g, b_g, o_g, wide)):
        rows = buf.shape[1]
        for t in range(dims[q][0] // rows):
            slot = step % slots
            if slot in pending:
                pending.pop(slot).wait()
            rr = pl.ds(t * rows, rows)
            scale = a[rr, :]
            for c in range(dims[q][1] // 128):
                cc = pl.ds(c * 128, 128)
                off = c * dims[q][0] + t * rows
                g, w = (ref[pl.ds(k * size + off, rows), :] for ref, k in where[q])
                buf[slot, :, cc] = w - (g * scale) * b[:, cc]
            cp = pltpu.make_async_copy(buf.at[slot], o.at[rr, :], o_sem.at[slot])
            cp.start()
            pending[slot] = cp
            step += 1
    for cp in pending.values():
        cp.wait()
    for c in small:
        c.wait()


def solution(mesh):
    def local_program(x_in, h_act, d_gate, d_up, d_out, w_gate, w_up, w_down, r_gate, c_gate, r_up, c_up, r_down, c_down, beta_two, rel_step, clip_thr):
        (mg, ng), (md, nd) = w_gate.shape, w_down.shape
        tokens = x_in.shape[0]
        nk = tokens // KB
        def hbm(*arrays):
            return tuple(pltpu.with_memory_space_constraint(v, HB) for v in arrays)

        def vmem(*arrays):
            return tuple(pltpu.with_memory_space_constraint(v, VM) for v in arrays)

        one = tuple(v.reshape(1, 1) for v in (beta_two, rel_step, clip_thr))
        dims = [(mg, ng), (mg, ng), (md, nd)]
        mm, nn = max(mg, md), max(ng, nd)
        dma = pltpu.SemaphoreType.DMA
        blocks = ng // 128 + nd // 128

        def call(kernel, outs, args, in_spaces, out_space, scratch, **params):
            return pl.pallas_call(
                functools.partial(kernel, dims),
                out_shape=outs,
                in_specs=[pl.BlockSpec(memory_space=v) for v in in_spaces],
                out_specs=tuple(pl.BlockSpec(memory_space=out_space) for _ in outs),
                scratch_shapes=scratch,
                compiler_params=pltpu.CompilerParams(vmem_limit_bytes=GRANT * 2**20, **params),
                name=kernel.__name__,
            )(*args)

        def vm(shapes):
            return tuple(VM(s, F32) for s in shapes)

        def vm(shapes):
            return tuple(VM(s, F32) for s in shapes)

        held_shape = (3 * mg * ng // 128, 128)
        lanes = [(m, 128) for m, _ in dims]
        stats = [s for m, n in dims for s in ((1, m), (1, n))]
        first = call(
            dot_kernel,
            vm([held_shape]) + (VM((md, tokens), BF16), VM((nd // NT, tokens, NT), BF16))
            + vm(lanes[:2] + [(8, ng), (8, ng), (8, 128), (3, 1, mm), (3, 1, nn)]),
            hbm(x_in, h_act, d_gate, d_up, d_out, w_gate, r_gate, c_gate, r_up, c_up, r_down, c_down), [HB] * 12, VM,
            [
                VM((nk, KB, mg), BF16), VM((3, KB, md), BF16), VM((mg, tokens), BF16), VM((RING, tokens, NT), BF16),
                dma((nk,)), dma((3,)), dma((RING,)), dma((nk,)), dma((nd // NT,)), dma((ng // 128,)), dma((6,)),
            ])
        second = call(
            exchange_kernel,
            vm([held_shape] + lanes + [(1, n) for _, n in dims] + stats),
            vmem(*first) + hbm(w_up, w_down) + one, [VM] * len(first) + [HB] * 2 + [pltpu.SMEM] * 3, VM,
            [
                VM((md, 128), F32), VM((8, nd), F32), VM((3, 8, 128), F32), VM((3, 8, 128), F32),
                VM((3, 1, mm), F32), VM((3, 1, mm), F32), VM((3, 1, nn), F32), VM((3, 3, 1, nn), F32),
                VM((16, 128), F32), VM((7, 16, 128), F32), dma((blocks,)),
                dma((3,)), dma((3,)), dma((3, 3)), dma((3, 3)), dma((7,)), dma((7,)),
            ], collective_id=0, has_side_effects=True)
        outs = call(
            write_kernel,
            tuple(jax.ShapeDtypeStruct(s, F32) for s in dims + [(k,) for mn in dims for k in mn]),
            vmem(*first, *second), [VM] * (len(first) + len(second)), HB,
            [VM((8, mg // 8, ng), F32), VM((8, md // 8, nd), F32), dma((8,)), dma((6,))])
        return tuple(outs)

    act_spec = P(None, "row")
    cot_spec = P(None, "col")
    w_spec = P("row", "col")
    r_spec = P("row")
    c_spec = P("col")
    s_spec = P()
    return jax.shard_map(local_program, mesh=mesh, in_specs=(act_spec, act_spec, cot_spec, cot_spec, cot_spec, w_spec, w_spec, w_spec, r_spec, c_spec, r_spec, c_spec, r_spec, c_spec, s_spec, s_spec, s_spec), out_specs=(w_spec, w_spec, w_spec, r_spec, c_spec, r_spec, c_spec, r_spec, c_spec), check_vma=False)
```

time: 49.5 us -> 52 us (1.051)
  Pallas kernels: 46.5 us -> 49.1 us
    pallas_call x3, Pallas kernels: 46.5 us -> 49.1 us  [call(): pl.pallas_call(functools.partial(kernel, dims), out_shape=outs, in_specs=...]
where the time goes in v4:
time: 52 us; the launch traced here: 51.9 us
  Pallas kernels  49.1 us (94%)
  between operations  2.76 us (5%)
    pallas_call x3, Pallas kernels, call(): pl.pallas_call(functools.partial(kernel, dims), out_shape=outs, in_specs=...  49.1 us

profile of v4, /device:TPU:0, one launch (start us, length us, event | category | flops | bytes accessed | tf_op | source)
XLA Modules:
  0.0 51.9 jit_solution(58698976653703634)
XLA Ops:
  2.6 17.3 %dot_kernel.1 = (f32[33792,128]{1,0:T(8,128)S(1)}, bf16[1408,2048]{1,0:T(8,128)(2,1)S(1)}, bf16[4,2048,256]{2,1,0:T(8,128)(2,1)S(1)}, f32[512,128]{1,0:T(8,128)S...) custom-call(bf16[2048,512]{1,0:T(8,128)(2,1)} %x.1, ...), custom_call_target="tpu_custom_call" | custom-call | tf_op jit(solution)/shard_map/dot_kernel/pallas_call | solution.py:420
  19.9 25.6 %exchange_kernel.1 = (f32[33792,128]{1,0:T(8,128)S(1)}, f32[512,128]{1,0:T(8,128)S(1)}, f32[512,128]{1,0:T(8,128)S(1)}, f32[1408,128]{1,0:T(8,128)S(1)}, f32[1,2...) custom-call(f32[33792,128]{1,0:T(8,128)S(1)} %get-tuple-element.32.h, ...), custom_call_target="tpu_custom_call" | custom-call | tf_op jit(solution)/shard_map/exchange_kernel/pallas_call | solution.py:420
  45.5 6.2 %write_kernel.1 = (f32[512,2816]{1,0:T(8,128)}, f32[512,2816]{1,0:T(8,128)}, f32[1408,1024]{1,0:T(8,128)}, f32[512]{0:T(512)}, f32[2816]{0:T(1024)}, /*index=5*/...) custom-call(f32[33792,128]{1,0:T(8,128)S(1)} %get-tuple-element.32.held, ...), custom_call_target="tpu_custom_call" | custom-call | tf_op jit(solution)/shard_map/write_kernel/pallas_call | solution.py:420

commit v5 on v4

v5 whole, which is shorter than its diff:
```python
import functools

import jax
import jax.numpy as jnp
from jax import lax
from jax.experimental import pallas as pl
from jax.experimental.pallas import tpu as pltpu
from jax.sharding import PartitionSpec as P

EPS_SQ = 1e-30
EPS_SCALE = 1e-3
F32 = jnp.float32
BF16 = jnp.bfloat16
MESH = pl.DeviceIdType.MESH
VM = pltpu.VMEM
HB = pltpu.HBM
KB = 256
NT = 256
WIDE = 2 * NT
HB_ROWS = 512
RING = 5
PIECES = (128, 128)
GRANT = 18
CHUNKS = 4


def fold(v):
    slabs = v.reshape(-1, 8, v.shape[1])
    n = slabs.shape[0] // 4 * 4
    s = jnp.sum(slabs[:n].reshape(-1, 4, 8, v.shape[1]), axis=0)
    s = (s[0] + s[1]) + (s[2] + s[3])
    for i in range(n, slabs.shape[0]):
        s = s + slabs[i]
    return s


def dot_kernel(
    dims,
    x, h, dg, du, dd, wgh, wuh, wdh, rg, cg, ru, cu, rd, cd,
    held, ht, dt, wg, wu, wd, rs_g, rs_u, cs_g, cs_u, sw, ro, co,
    xs, hs, xt, ring, x_sem, h_sem, d_sem, first_sem, big_sem, s_sem,
):
    m, n = dims[0]
    nk = x.shape[0] // KB
    up = n // NT
    cots, rss, css = (dg, du), (rs_g, rs_u), (cs_g, cs_u)
    n_units = 2 * up
    tiles, unit_tile = [], []
    for q in range(2):
        for c0 in range(0, n, WIDE):
            cols = min(WIDE, n - c0)
            for off in range(0, cols, NT):
                unit_tile.append((len(tiles), off))
            tiles.append((q, c0, cols))

    def x_copy(k):
        return pltpu.make_async_copy(x.at[pl.ds(k * KB, KB), :], xs.at[k], x_sem.at[k])

    def first_copy(k):
        return pltpu.make_async_copy(dg.at[pl.ds(k * KB, KB), pl.ds(0, WIDE)], ring.at[0, pl.ds(k * KB, KB), :], first_sem.at[k])

    def d_copy(t):
        q, c0, cols = tiles[t]
        return pltpu.make_async_copy(cots[q].at[:, pl.ds(c0, cols)], ring.at[t % RING, :, pl.ds(0, cols)], d_sem.at[t % RING])

    def h_copy(k):
        return pltpu.make_async_copy(h.at[pl.ds(k * HB_ROWS, HB_ROWS), :], hs.at[k % 2], h_sem.at[k % 2])

    bigs = [pltpu.make_async_copy(a, b, big_sem.at[i]) for i, (a, b) in enumerate(((wgh, wg), (dd, dt), (wuh, wu), (wdh, wd)))]
    small = [
        pltpu.make_async_copy(src, dst.at[q, 0, pl.ds(0, src.shape[0])], s_sem.at[i])
        for i, (src, dst, q) in enumerate(
            [(rg, ro, 0), (ru, ro, 1), (rd, ro, 2), (cg, co, 0), (cu, co, 1), (cd, co, 2)])
    ]
    for k in range(nk):
        x_copy(k).start()
        first_copy(k).start()

    blocks = ht.shape[0] // 128

    def h_turn(k, part):
        for c in range(part * (blocks // 2), blocks if part else blocks // 2):
            ht[pl.ds(c * 128, 128), pl.ds(k * HB_ROWS, HB_ROWS)] = hs[k % 2, :, pl.ds(c * 128, 128)].T

    def w_square(c):
        w = wg[:, pl.ds(c * 128, 128)]
        s = fold(w * w)
        if c == 0:
            sw[...] = s
        else:
            sw[...] += s

    before = {u: [] for u in range(n_units)}
    beside = [[] for _ in range(n_units)]
    before[1] += [h_copy(0).start, h_copy(1).start]
    before[3] += [h_copy(0).wait]
    before[5] += [h_copy(1).wait, h_copy(2).start]
    before[7] += [h_copy(2).wait, h_copy(3).start]
    before[9] += [h_copy(3).wait]
    for k in range(4):
        for part in range(2):
            beside[3 + 2 * k + part].append(lambda k=k, part=part: h_turn(k, part))
    before[7].append(bigs[0].start)
    before[10].append(bigs[1].start)
    before[12].append(bigs[2].start)
    before[14].append(bigs[3].start)
    before[16].append(bigs[0].wait)
    for c in range(n // 128):
        beside[16 + c // 5].append(lambda c=c: w_square(c))

    def run(*accs):
        def acc(z, par, p):
            return accs[(z * 2 + par) * 2 + p]

        def rhs(u, k):
            t, off = unit_tile[u]
            return ring[t % RING, pl.ds(k * KB, KB), pl.ds(off, NT)]

        def drain(u):
            q, j = divmod(u, up)
            cc = None
            for z in range(2):
                for p, size in enumerate(PIECES):
                    r0 = z * sum(PIECES) + sum(PIECES[:p])
                    g = pltpu.matmul_pop(acc(z, u % 2, p))
                    for half in range(2):
                        held[pl.ds((q * (n // 128) + 2 * j + half) * m + r0, size), :] = g[:, half * 128:half * 128 + 128]
                    s = g * g
                    lanes = s[:, :128] + s[:, 128:]
                    if j == 0:
                        rss[q][pl.ds(r0, size), :] = lanes
                    else:
                        rss[q][pl.ds(r0, size), :] += lanes
                    s = fold(s)
                    cc = s if cc is None else cc + s
            css[q][:, pl.ds(j * NT, NT)] = cc

        for z in range(2):
            for par in range(2):
                for p in range(2):
                    pltpu.matmul_pop(acc(z, par, p))

        for u in range(n_units):
            last = u == n_units - 1
            t = unit_tile[u][0]
            if not last and unit_tile[u + 1][0] != t:
                d_copy(t + 1).wait()
                if t and t - 1 + RING < len(tiles):
                    d_copy(t - 1 + RING).start()
                for f in before.pop(u):
                    f()
            for k in range(nk):
                if u == 0:
                    x_copy(k).wait()
                    first_copy(k).wait()
                    for z in range(2):
                        xt[pl.ds(z * 256, 256), pl.ds(k * KB, KB)] = xs[k, :, pl.ds(z * 256, 256)].T
                        pltpu.matmul_push_rhs(rhs(0, k), staging_register=k % 2, mxu_index=z)
                    if k % 2 == 0 and k // 2 + 1 < RING:
                        d_copy(k // 2 + 1).start()
                for z in range(2):
                    for p, size in enumerate(PIECES):
                        r0 = z * sum(PIECES) + sum(PIECES[:p])
                        pltpu.matmul_acc_lhs(acc(z, u % 2, p), xt[pl.ds(r0, size), pl.ds(k * KB, KB)],
                                             load_staged_rhs=(k % 2 if p == 0 else None))
                    if k < nk - 1:
                        if u:
                            pltpu.matmul_push_rhs(rhs(u, k + 1), staging_register=(k + 1) % 2, mxu_index=z)
                    elif not last:
                        pltpu.matmul_push_rhs(rhs(u + 1, 0), staging_register=0, mxu_index=z)
                if k == 1 and u:
                    drain(u - 1)
                if k == 2:
                    for f in beside[u]:
                        f()
        drain(n_units - 1)
        assert not any(before.values())

    for c in small:
        c.start()
    pl.run_scoped(run, *[pltpu.ACC(z)((size, NT), F32) for z in range(2) for par in range(2) for size in PIECES])
    for c in bigs[1:] + small:
        c.wait()


def exchange_kernel(
    dims,
    held, ht, dt, wg, wu, wd, rs_g, rs_u, cs_g, cs_u, sw_g, ro, co,
    b2, rel, clip,
    late, a_g, a_u, a_d, b_g, b_u, b_d, r_g, c_g, r_u, c_u, r_d, c_d,
    rs_d, cs_d, su, sw, rsend, rrecv, csend, crecv, pay, got, pay2, got2, r1s, r1r, c1s, c1r, p_s, p_r, p2_s, p2_r,
):
    col = lax.axis_index("col")
    row = lax.axis_index("row")
    row_peer = (row + 1 - 2 * (row % 2), (row + 2) % 4, 3 - row)
    mats = (
        dict(rs=rs_g, cs=cs_g, a=a_g, b=b_g, r=r_g, c=c_g),
        dict(rs=rs_u, cs=cs_u, a=a_u, b=b_u, r=r_u, c=c_u),
        dict(rs=rs_d, cs=cs_d, a=a_d, b=b_d, r=r_d, c=c_d),
    )
    for mat, (m, n) in zip(mats, dims):
        mat["m"], mat["n"] = m, n
        mat["mt"], mat["nt"] = m * 4, n * 2
    (mg, ng), (md, nd) = dims[0], dims[2]
    size = mg * ng // 128

    barrier = pltpu.get_barrier_semaphore()
    plane = [{"row": p, "col": cc} for cc in (col, 1 - col) for p in (row,) + row_peer][1:]
    for dev in plane:
        pl.semaphore_signal(barrier, inc=1, device_id=dev, device_id_type=MESH)

    pay[...] = jnp.zeros_like(pay)
    pay2[...] = jnp.zeros_like(pay2)

    def w_square(q, w):
        m, n = dims[q]
        sw[...] = jnp.zeros_like(sw)

        @pl.loop(0, n // 256)
        def _(c):
            c0 = pl.multiple_of(c * 256, 256)
            a, b = w[:, pl.ds(c0, 128)], w[:, pl.ds(c0 + 128, 128)]
            sw[...] += fold(a * a) + fold(b * b)

        pay[pl.ds(q, 1), :] = jnp.sum(sw[...], axis=0, keepdims=True)

    def first_sends(q):
        mat = mats[q]
        m, n = mat["m"], mat["n"]
        copies = [pltpu.make_async_remote_copy(
            rsend.at[q, :, pl.ds(0, m)], rrecv.at[q, :, pl.ds(0, m)], r1s.at[q], r1r.at[q],
            device_id={"col": 1 - col}, device_id_type=MESH)]
        for d in range(3):
            copies.append(pltpu.make_async_remote_copy(
                csend.at[q, :, pl.ds(0, n)], crecv.at[q, d, :, pl.ds(0, n)], c1s.at[q, d], c1r.at[q, d],
                device_id={"row": row_peer[d]}, device_id_type=MESH))
        return copies

    def first_reduce(q):
        mat = mats[q]
        csend[q, :, pl.ds(0, mat["n"])] = jnp.sum(mat["cs"][...], axis=0, keepdims=True)
        for b in range(mat["m"] // 128):
            t = mat["rs"][pl.ds(b * 128, 128), :].T
            rsend[q, :, pl.ds(b * 128, 128)] = jnp.sum(t, axis=0, keepdims=True)

    def new_stats(q):
        mat = mats[q]
        m, n = mat["m"], mat["n"]
        beta = b2[0, 0]
        rsum = rsend[q, :, pl.ds(0, m)] + rrecv[q, :, pl.ds(0, m)]
        r_new = beta * ro[q, :, pl.ds(0, m)] + (1.0 - beta) * (rsum * (1.0 / mat["nt"]) + EPS_SQ)
        mat["r"][...] = r_new
        csum = (csend[q, :, pl.ds(0, n)] + crecv[q, 0, :, pl.ds(0, n)]) + (
            crecv[q, 1, :, pl.ds(0, n)] + crecv[q, 2, :, pl.ds(0, n)])
        c_new = beta * co[q, :, pl.ds(0, n)] + (1.0 - beta) * (csum * (1.0 / mat["mt"]) + EPS_SQ)
        mat["c"][...] = c_new
        mat["b"][...] = lax.rsqrt(c_new)
        alpha = lax.rsqrt(r_new)
        rp = r_new[:, :128]
        for b in range(m // 128):
            blk = jnp.broadcast_to(alpha[:, b * 128:(b + 1) * 128], (128, 128))
            mat["a"][pl.ds(b * 128, 128), :] = blk.T
            if b:
                rp = rp + r_new[:, b * 128:(b + 1) * 128]
        if q == 2:
            pay2[pl.ds(3, 1), :] = rp
        else:
            pay[pl.ds(3 + q, 1), :] = rp

    def u_square(q):
        mat = mats[q]
        m = mat["m"]
        src, first = (late, 0) if q == 2 else (held, q * size)
        su[...] = jnp.zeros_like(su)

        @pl.loop(0, mat["n"] // 256)
        def _(c):
            total = None
            for half in range(2):
                c0 = pl.multiple_of(c * 256 + half * 128, 128)
                g = src[pl.ds(pl.multiple_of(first + (2 * c + half) * m, 128), m), :]
                t = g * mat["a"][...]
                bb = mat["b"][:, pl.ds(c0, 128)]
                s = fold(t * t) * (bb * bb)
                total = s if total is None else total + s
            su[...] += total

        pay2[pl.ds(q, 1), :] = jnp.sum(su[...], axis=0, keepdims=True)

    rows = md // CHUNKS
    steps = nd // NT * CHUNKS

    def product(i):
        j, c = divmod(i, CHUNKS)
        rr = pl.ds(c * rows, rows)
        g = jnp.dot(ht[rr, :], dt[:, pl.ds(j * NT, NT)], preferred_element_type=F32)
        for half in range(2):
            late[pl.ds((2 * j + half) * md + c * rows, rows), :] = g[:, half * 128:half * 128 + 128]
        s = g * g
        lanes = s[:, :128] + s[:, 128:]
        if j == 0:
            rs_d[rr, :] = lanes
        else:
            rs_d[rr, :] += lanes
        cc = pl.ds(j * NT, NT)
        if c == 0:
            cs_d[:, cc] = fold(s)
        else:
            cs_d[:, cc] += fold(s)

    def plane_sends(src, dst, rows, s_sem, r_sem):
        rr = pl.ds(0, rows)
        return [pltpu.make_async_remote_copy(src.at[rr], dst.at[i, rr], s_sem.at[i], r_sem.at[i], device_id=dev, device_id_type=MESH)
                for i, dev in enumerate(plane)]

    def plane_sum(src, dst, rows):
        a = [src[pl.ds(0, rows), :]] + [dst[i, pl.ds(0, rows), :] for i in range(len(plane))]
        total = ((a[0] + a[1]) + (a[2] + a[3])) + ((a[4] + a[5]) + (a[6] + a[7]))
        return jnp.sum(total, axis=1, keepdims=True)

    early = [c for q in range(2) for c in first_sends(q)]
    for i in range(steps):
        if i == CHUNKS:
            first_reduce(0)
            first_reduce(1)
            pl.semaphore_wait(barrier, len(plane))
            for c in early:
                c.start()
        product(i)
    first_reduce(2)
    sends = first_sends(2)
    for c in sends:
        c.start()
    for c in early:
        c.wait()
    pay[pl.ds(0, 1), :] = jnp.sum(sw_g[...], axis=0, keepdims=True)
    for q in range(2):
        new_stats(q)
    w_square(1, wu)
    w_square(2, wd)
    sums = plane_sends(pay, got, 5, p_s, p_r)
    for c in sums:
        c.start()
    for q in range(2):
        u_square(q)
    for c in sends:
        c.wait()
    new_stats(2)
    u_square(2)
    sums2 = plane_sends(pay2, got2, 4, p2_s, p2_r)
    for c in sums2:
        c.start()
    for c in sums + sums2:
        c.wait()
    norms = plane_sum(pay, got, 5)
    shapes = plane_sum(pay2, got2, 4)
    for q, mat in enumerate(mats):
        count = float(mat["mt"] * mat["nt"])
        r_sum = shapes[3:4] if q == 2 else norms[3 + q:4 + q]
        r_mean = r_sum * (0.5 / mat["mt"])
        u_rms = jnp.sqrt(r_mean * shapes[q:q + 1] / count)
        w_rms = jnp.sqrt(norms[q:q + 1] / count)
        step = rel[0, 0] * jnp.maximum(EPS_SCALE, w_rms)
        k = step * jnp.sqrt(r_mean) / jnp.maximum(1.0, u_rms / clip[0, 0])
        mat["b"][...] = mat["b"][...] * k


def write_kernel(
    dims,
    held, ht, dt, w_g, w_u, w_d, rs_g, rs_u, cs_g, cs_u, sw_g, ro, co,
    late, a_g, a_u, a_d, b_g, b_u, b_d, r_g, c_g, r_u, c_u, r_d, c_d,
    o_g, o_u, o_d, or_g, oc_g, or_u, oc_u, or_d, oc_d,
    wide, tall, o_sem, s_sem,
):
    small = [pltpu.make_async_copy(s.at[0], d, s_sem.at[i]) for i, (s, d) in enumerate(
        [(r_g, or_g), (c_g, oc_g), (r_u, or_u), (c_u, oc_u), (r_d, or_d), (c_d, oc_d)])]
    for c in small:
        c.start()
    slots = 8
    size = dims[0][0] * dims[0][1] // 128
    where = ((held, 0, w_g), (held, 1, w_u), (late, 0, w_d))
    pending = {}
    step = 0
    for q, a, b, o, buf in ((2, a_d, b_d, o_d, tall), (1, a_u, b_u, o_u, wide), (0, a_g, b_g, o_g, wide)):
        rows = buf.shape[1]
        src, k, w = where[q]
        for t in range(dims[q][0] // rows):
            slot = step % slots
            if slot in pending:
                pending.pop(slot).wait()
            rr = pl.ds(t * rows, rows)
            scale = a[rr, :]
            for c in range(dims[q][1] // 128):
                cc = pl.ds(c * 128, 128)
                off = c * dims[q][0] + t * rows
                g = src[pl.ds(k * size + off, rows), :]
                buf[slot, :, cc] = w[rr, cc] - (g * scale) * b[:, cc]
            cp = pltpu.make_async_copy(buf.at[slot], o.at[rr, :], o_sem.at[slot])
            cp.start()
            pending[slot] = cp
            step += 1
    for cp in pending.values():
        cp.wait()
    for c in small:
        c.wait()


def solution(mesh):
    def local_program(x_in, h_act, d_gate, d_up, d_out, w_gate, w_up, w_down, r_gate, c_gate, r_up, c_up, r_down, c_down, beta_two, rel_step, clip_thr):
        (mg, ng), (md, nd) = w_gate.shape, w_down.shape
        tokens = x_in.shape[0]
        nk = tokens // KB
        def hbm(*arrays):
            return tuple(pltpu.with_memory_space_constraint(v, HB) for v in arrays)

        def vmem(*arrays):
            return tuple(pltpu.with_memory_space_constraint(v, VM) for v in arrays)

        one = tuple(v.reshape(1, 1) for v in (beta_two, rel_step, clip_thr))
        dims = [(mg, ng), (mg, ng), (md, nd)]
        mm, nn = max(mg, md), max(ng, nd)
        dma = pltpu.SemaphoreType.DMA

        def call(kernel, outs, args, in_spaces, out_space, scratch, **params):
            return pl.pallas_call(
                functools.partial(kernel, dims),
                out_shape=outs,
                in_specs=[pl.BlockSpec(memory_space=v) for v in in_spaces],
                out_specs=tuple(pl.BlockSpec(memory_space=out_space) for _ in outs),
                scratch_shapes=scratch,
                compiler_params=pltpu.CompilerParams(vmem_limit_bytes=GRANT * 2**20, **params),
                name=kernel.__name__,
            )(*args)

        def vm(shapes):
            return tuple(VM(s, F32) for s in shapes)

        def vm(shapes):
            return tuple(VM(s, F32) for s in shapes)

        size = mg * ng // 128
        lanes = [(m, 128) for m, _ in dims]
        stats = [s for m, n in dims for s in ((1, m), (1, n))]
        first = call(
            dot_kernel,
            vm([(2 * size, 128)]) + (VM((md, tokens), BF16), VM((tokens, nd), BF16))
            + vm(dims + lanes[:2] + [(8, ng), (8, ng), (8, 128), (3, 1, mm), (3, 1, nn)]),
            hbm(x_in, h_act, d_gate, d_up, d_out, w_gate, w_up, w_down, r_gate, c_gate, r_up, c_up, r_down, c_down), [HB] * 14, VM,
            [
                VM((nk, KB, mg), BF16), VM((2, HB_ROWS, md), BF16), VM((mg, tokens), BF16), VM((RING, tokens, WIDE), BF16),
                dma((nk,)), dma((2,)), dma((RING,)), dma((nk,)), dma((4,)), dma((6,)),
            ])
        second = call(
            exchange_kernel,
            vm([(size, 128)] + lanes + [(1, n) for _, n in dims] + stats),
            vmem(*first) + one, [VM] * len(first) + [pltpu.SMEM] * 3, VM,
            [
                VM((md, 128), F32), VM((8, nd), F32), VM((8, 128), F32), VM((8, 128), F32),
                VM((3, 1, mm), F32), VM((3, 1, mm), F32), VM((3, 1, nn), F32), VM((3, 3, 1, nn), F32),
                VM((8, 128), F32), VM((7, 8, 128), F32), VM((8, 128), F32), VM((7, 8, 128), F32),
                dma((3,)), dma((3,)), dma((3, 3)), dma((3, 3)), dma((7,)), dma((7,)), dma((7,)), dma((7,)),
            ], collective_id=0, has_side_effects=True)
        outs = call(
            write_kernel,
            tuple(jax.ShapeDtypeStruct(s, F32) for s in dims + [(k,) for mn in dims for k in mn]),
            vmem(*first, *second), [VM] * (len(first) + len(second)), HB,
            [VM((8, mg // 8, ng), F32), VM((8, md // 8, nd), F32), dma((8,)), dma((6,))])
        return tuple(outs)

    act_spec = P(None, "row")
    cot_spec = P(None, "col")
    w_spec = P("row", "col")
    r_spec = P("row")
    c_spec = P("col")
    s_spec = P()
    return jax.shard_map(local_program, mesh=mesh, in_specs=(act_spec, act_spec, cot_spec, cot_spec, cot_spec, w_spec, w_spec, w_spec, r_spec, c_spec, r_spec, c_spec, r_spec, c_spec, s_spec, s_spec, s_spec), out_specs=(w_spec, w_spec, w_spec, r_spec, c_spec, r_spec, c_spec, r_spec, c_spec), check_vma=False)
```

time: 52 us -> 45.6 us (0.88)
  Pallas kernels: 49.1 us -> 42.7 us
    pallas_call x3, Pallas kernels: 49.1 us -> 42.7 us  [call(): pl.pallas_call(functools.partial(kernel, dims), out_shape=outs, in_specs=...]
where the time goes in v5:
time: 45.6 us; the launch traced here: 45.5 us
  Pallas kernels  42.7 us (94%)
  between operations  2.76 us (6%)
    pallas_call x3, Pallas kernels, call(): pl.pallas_call(functools.partial(kernel, dims), out_shape=outs, in_specs=...  42.7 us

profile of v5, /device:TPU:0, one launch (start us, length us, event | category | flops | bytes accessed | tf_op | source)
XLA Modules:
  0.0 45.5 jit_solution(13908132630011364671)
XLA Ops:
  2.6 18.8 %dot_kernel.1 = (f32[22528,128]{1,0:T(8,128)S(1)}, bf16[1408,2048]{1,0:T(8,128)(2,1)S(1)}, bf16[2048,1024]{1,0:T(8,128)(2,1)S(1)}, f32[512,2816]{1,0:T(8,128)S(1...) custom-call(bf16[2048,512]{1,0:T(8,128)(2,1)} %x.1, ...), custom_call_target="tpu_custom_call" | custom-call | tf_op jit(solution)/shard_map/dot_kernel/pallas_call | solution.py:425
  21.4 17.6 %exchange_kernel.1 = (f32[11264,128]{1,0:T(8,128)S(1)}, f32[512,128]{1,0:T(8,128)S(1)}, f32[512,128]{1,0:T(8,128)S(1)}, f32[1408,128]{1,0:T(8,128)S(1)}, f32[1,2...) custom-call(f32[22528,128]{1,0:T(8,128)S(1)} %get-tuple-element.35.h, ...), custom_call_target="tpu_custom_call" | custom-call | tf_op jit(solution)/shard_map/exchange_kernel/pallas_call | solution.py:425
  39.0 6.3 %write_kernel.1 = (f32[512,2816]{1,0:T(8,128)}, f32[512,2816]{1,0:T(8,128)}, f32[1408,1024]{1,0:T(8,128)}, f32[512]{0:T(512)}, f32[2816]{0:T(1024)}, /*index=5*/...) custom-call(f32[22528,128]{1,0:T(8,128)S(1)} %get-tuple-element.35.held, ...), custom_call_target="tpu_custom_call" | custom-call | tf_op jit(solution)/shard_map/write_kernel/pallas_call | solution.py:425

commit v6 on v5

--- a/solution.py
+++ b/solution.py
@@ -36,8 +36,8 @@
 
 def dot_kernel(
     dims,
-    x, h, dg, du, dd, wgh, wuh, wdh, rg, cg, ru, cu, rd, cd,
-    held, ht, dt, wg, wu, wd, rs_g, rs_u, cs_g, cs_u, sw, ro, co,
+    x, h, dg, du, dd, wgh, rg, cg, ru, cu, rd, cd,
+    held, ht, dt, wg, rs_g, rs_u, cs_g, cs_u, sw, ro, co,
     xs, hs, xt, ring, x_sem, h_sem, d_sem, first_sem, big_sem, s_sem,
 ):
     m, n = dims[0]
@@ -66,7 +66,7 @@
     def h_copy(k):
         return pltpu.make_async_copy(h.at[pl.ds(k * HB_ROWS, HB_ROWS), :], hs.at[k % 2], h_sem.at[k % 2])
 
-    bigs = [pltpu.make_async_copy(a, b, big_sem.at[i]) for i, (a, b) in enumerate(((wgh, wg), (dd, dt), (wuh, wu), (wdh, wd)))]
+    bigs = [pltpu.make_async_copy(a, b, big_sem.at[i]) for i, (a, b) in enumerate(((wgh, wg), (dd, dt)))]
     small = [
         pltpu.make_async_copy(src, dst.at[q, 0, pl.ds(0, src.shape[0])], s_sem.at[i])
         for i, (src, dst, q) in enumerate(
@@ -102,8 +102,6 @@
             beside[3 + 2 * k + part].append(lambda k=k, part=part: h_turn(k, part))
     before[7].append(bigs[0].start)
     before[10].append(bigs[1].start)
-    before[12].append(bigs[2].start)
-    before[14].append(bigs[3].start)
     before[16].append(bigs[0].wait)
     for c in range(n // 128):
         beside[16 + c // 5].append(lambda c=c: w_square(c))
@@ -185,10 +183,11 @@
 
 def exchange_kernel(
     dims,
-    held, ht, dt, wg, wu, wd, rs_g, rs_u, cs_g, cs_u, sw_g, ro, co,
+    held, ht, dt, wg, rs_g, rs_u, cs_g, cs_u, sw_g, ro, co,
+    wuh, wdh,
     b2, rel, clip,
-    late, a_g, a_u, a_d, b_g, b_u, b_d, r_g, c_g, r_u, c_u, r_d, c_d,
-    rs_d, cs_d, su, sw, rsend, rrecv, csend, crecv, pay, got, pay2, got2, r1s, r1r, c1s, c1r, p_s, p_r, p2_s, p2_r,
+    late, wu, wd, a_g, a_u, a_d, b_g, b_u, b_d, r_g, c_g, r_u, c_u, r_d, c_d,
+    w_sem, rs_d, cs_d, su, sw, rsend, rrecv, csend, crecv, pay, got, pay2, got2, r1s, r1r, c1s, c1r, p_s, p_r, p2_s, p2_r,
 ):
     col = lax.axis_index("col")
     row = lax.axis_index("row")
@@ -209,6 +208,9 @@
     for dev in plane:
         pl.semaphore_signal(barrier, inc=1, device_id=dev, device_id_type=MESH)
 
+    loads = [pltpu.make_async_copy(a, b, w_sem.at[i]) for i, (a, b) in enumerate(((wuh, wu), (wdh, wd)))]
+    for c in loads:
+        c.start()
     pay[...] = jnp.zeros_like(pay)
     pay2[...] = jnp.zeros_like(pay2)
 
@@ -336,6 +338,8 @@
     pay[pl.ds(0, 1), :] = jnp.sum(sw_g[...], axis=0, keepdims=True)
     for q in range(2):
         new_stats(q)
+    for c in loads:
+        c.wait()
     w_square(1, wu)
     w_square(2, wd)
     sums = plane_sends(pay, got, 5, p_s, p_r)
@@ -367,8 +371,8 @@
 
 def write_kernel(
     dims,
-    held, ht, dt, w_g, w_u, w_d, rs_g, rs_u, cs_g, cs_u, sw_g, ro, co,
-    late, a_g, a_u, a_d, b_g, b_u, b_d, r_g, c_g, r_u, c_u, r_d, c_d,
+    held, ht, dt, w_g, rs_g, rs_u, cs_g, cs_u, sw_g, ro, co,
+    late, w_u, w_d, a_g, a_u, a_d, b_g, b_u, b_d, r_g, c_g, r_u, c_u, r_d, c_d,
     o_g, o_u, o_d, or_g, oc_g, or_u, oc_u, or_d, oc_d,
     wide, tall, o_sem, s_sem,
 ):
@@ -444,17 +448,18 @@
         first = call(
             dot_kernel,
             vm([(2 * size, 128)]) + (VM((md, tokens), BF16), VM((tokens, nd), BF16))
-            + vm(dims + lanes[:2] + [(8, ng), (8, ng), (8, 128), (3, 1, mm), (3, 1, nn)]),
-            hbm(x_in, h_act, d_gate, d_up, d_out, w_gate, w_up, w_down, r_gate, c_gate, r_up, c_up, r_down, c_down), [HB] * 14, VM,
+            + vm(dims[:1] + lanes[:2] + [(8, ng), (8, ng), (8, 128), (3, 1, mm), (3, 1, nn)]),
+            hbm(x_in, h_act, d_gate, d_up, d_out, w_gate, r_gate, c_gate, r_up, c_up, r_down, c_down), [HB] * 12, VM,
             [
                 VM((nk, KB, mg), BF16), VM((2, HB_ROWS, md), BF16), VM((mg, tokens), BF16), VM((RING, tokens, WIDE), BF16),
-                dma((nk,)), dma((2,)), dma((RING,)), dma((nk,)), dma((4,)), dma((6,)),
+                dma((nk,)), dma((2,)), dma((RING,)), dma((nk,)), dma((2,)), dma((6,)),
             ])
         second = call(
             exchange_kernel,
-            vm([(size, 128)] + lanes + [(1, n) for _, n in dims] + stats),
-            vmem(*first) + one, [VM] * len(first) + [pltpu.SMEM] * 3, VM,
+            vm([(size, 128)] + dims[1:] + lanes + [(1, n) for _, n in dims] + stats),
+            vmem(*first) + hbm(w_up, w_down) + one, [VM] * len(first) + [HB] * 2 + [pltpu.SMEM] * 3, VM,
             [
+                dma((2,)),
                 VM((md, 128), F32), VM((8, nd), F32), VM((8, 128), F32), VM((8, 128), F32),
                 VM((3, 1, mm), F32), VM((3, 1, mm), F32), VM((3, 1, nn), F32), VM((3, 3, 1, nn), F32),
                 VM((8, 128), F32), VM((7, 8, 128), F32), VM((8, 128), F32), VM((7, 8, 128), F32),

time: 45.6 us -> 44.9 us (0.985)
  Pallas kernels: 42.7 us -> 42 us
    pallas_call x3, Pallas kernels: 42.7 us -> 42 us  [call(): pl.pallas_call(functools.partial(kernel, dims), out_shape=outs, in_specs=...]
where the time goes in v6:
time: 44.9 us; the launch traced here: 44.8 us
  Pallas kernels  42 us (94%)
  between operations  2.76 us (6%)
    pallas_call x3, Pallas kernels, call(): pl.pallas_call(functools.partial(kernel, dims), out_shape=outs, in_specs=...  42 us

profile of v6, /device:TPU:0, one launch (start us, length us, event | category | flops | bytes accessed | tf_op | source)
XLA Modules:
  0.0 44.8 jit_solution(15362024166182922938)
XLA Ops:
  2.6 18.1 %dot_kernel.1 = (f32[22528,128]{1,0:T(8,128)S(1)}, bf16[1408,2048]{1,0:T(8,128)(2,1)S(1)}, bf16[2048,1024]{1,0:T(8,128)(2,1)S(1)}, f32[512,2816]{1,0:T(8,128)S(1...) custom-call(bf16[2048,512]{1,0:T(8,128)(2,1)} %x.1, ...), custom_call_target="tpu_custom_call" | custom-call | tf_op jit(solution)/shard_map/dot_kernel/pallas_call | solution.py:429
  20.6 17.7 %exchange_kernel.1 = (f32[11264,128]{1,0:T(8,128)S(1)}, f32[512,2816]{1,0:T(8,128)S(1)}, f32[1408,1024]{1,0:T(8,128)S(1)}, f32[512,128]{1,0:T(8,128)S(1)}, f32[5...) custom-call(f32[22528,128]{1,0:T(8,128)S(1)} %get-tuple-element.35.h, ...), custom_call_target="tpu_custom_call" | custom-call | tf_op jit(solution)/shard_map/exchange_kernel/pallas_call | solution.py:429
  38.3 6.2 %write_kernel.1 = (f32[512,2816]{1,0:T(8,128)}, f32[512,2816]{1,0:T(8,128)}, f32[1408,1024]{1,0:T(8,128)}, f32[512]{0:T(512)}, f32[2816]{0:T(1024)}, /*index=5*/...) custom-call(f32[22528,128]{1,0:T(8,128)S(1)} %get-tuple-element.35.held, ...), custom_call_target="tpu_custom_call" | custom-call | tf_op jit(solution)/shard_map/write_kernel/pallas_call | solution.py:429

commit v7 on v6

--- a/solution.py
+++ b/solution.py
@@ -47,17 +47,19 @@
     n_units = 2 * up
     tiles, unit_tile = [], []
     for q in range(2):
-        for c0 in range(0, n, WIDE):
-            cols = min(WIDE, n - c0)
+        odd = n % WIDE
+        for c0, cols in ([(0, odd)] if odd and not q else []) + [(c, min(WIDE, n - c)) for c in range(0 if q else odd, n, WIDE)]:
             for off in range(0, cols, NT):
                 unit_tile.append((len(tiles), off))
             tiles.append((q, c0, cols))
 
+    wide0 = tiles[0][2]
+
     def x_copy(k):
         return pltpu.make_async_copy(x.at[pl.ds(k * KB, KB), :], xs.at[k], x_sem.at[k])
 
     def first_copy(k):
-        return pltpu.make_async_copy(dg.at[pl.ds(k * KB, KB), pl.ds(0, WIDE)], ring.at[0, pl.ds(k * KB, KB), :], first_sem.at[k])
+        return pltpu.make_async_copy(dg.at[pl.ds(k * KB, KB), pl.ds(0, wide0)], ring.at[0, pl.ds(k * KB, KB), pl.ds(0, wide0)], first_sem.at[k])
 
     def d_copy(t):
         q, c0, cols = tiles[t]
@@ -92,19 +94,25 @@
 
     before = {u: [] for u in range(n_units)}
     beside = [[] for _ in range(n_units)]
-    before[1] += [h_copy(0).start, h_copy(1).start]
-    before[3] += [h_copy(0).wait]
-    before[5] += [h_copy(1).wait, h_copy(2).start]
-    before[7] += [h_copy(2).wait, h_copy(3).start]
-    before[9] += [h_copy(3).wait]
-    for k in range(4):
+    heads = [u for u in range(n_units - 1) if unit_tile[u][0] != unit_tile[u + 1][0]]
+
+    def head(u):
+        return max(v for v in heads if v <= u)
+
+    wait_h = (head(7), head(9), head(15), head(17))
+    for u, k in zip((head(2), head(2), wait_h[1], head(wait_h[1] + 3)), range(4)):
+        before[u].append(h_copy(k).start)
+    for u, k in zip(wait_h, range(4)):
+        before[u].append(h_copy(k).wait)
         for part in range(2):
-            beside[3 + 2 * k + part].append(lambda k=k, part=part: h_turn(k, part))
-    before[7].append(bigs[0].start)
-    before[10].append(bigs[1].start)
-    before[16].append(bigs[0].wait)
+            beside[u + part].append(lambda k=k, part=part: h_turn(k, part))
+    before[head(11)].append(bigs[0].start)
+    before[head(14)].append(bigs[1].start)
+    w0 = head(19)
+    before[w0].append(bigs[0].wait)
+    span = n_units - w0
     for c in range(n // 128):
-        beside[16 + c // 5].append(lambda c=c: w_square(c))
+        beside[w0 + c * span // (n // 128)].append(lambda c=c: w_square(c))
 
     def run(*accs):
         def acc(z, par, p):
@@ -142,7 +150,8 @@
             last = u == n_units - 1
             t = unit_tile[u][0]
             if not last and unit_tile[u + 1][0] != t:
-                d_copy(t + 1).wait()
+                if u:
+                    d_copy(t + 1).wait()
                 if t and t - 1 + RING < len(tiles):
                     d_copy(t - 1 + RING).start()
                 for f in before.pop(u):
@@ -154,8 +163,10 @@
                     for z in range(2):
                         xt[pl.ds(z * 256, 256), pl.ds(k * KB, KB)] = xs[k, :, pl.ds(z * 256, 256)].T
                         pltpu.matmul_push_rhs(rhs(0, k), staging_register=k % 2, mxu_index=z)
-                    if k % 2 == 0 and k // 2 + 1 < RING:
+                    if k % 2 and k // 2 + 1 < RING:
                         d_copy(k // 2 + 1).start()
+                    if k == nk - 1 and unit_tile[1][0] == 1:
+                        d_copy(1).wait()
                 for z in range(2):
                     for p, size in enumerate(PIECES):
                         r0 = z * sum(PIECES) + sum(PIECES[:p])
@@ -187,7 +198,7 @@
     wuh, wdh,
     b2, rel, clip,
     late, wu, wd, a_g, a_u, a_d, b_g, b_u, b_d, r_g, c_g, r_u, c_u, r_d, c_d,
-    w_sem, rs_d, cs_d, su, sw, rsend, rrecv, csend, crecv, pay, got, pay2, got2, r1s, r1r, c1s, c1r, p_s, p_r, p2_s, p2_r,
+    w_sem, rs_d, cs_d, sw, rsend, rrecv, csend, crecv, pay, got, pay2, got2, r1s, r1r, c1s, c1r, p_s, p_r, p2_s, p2_r,
 ):
     col = lax.axis_index("col")
     row = lax.axis_index("row")
@@ -269,25 +280,28 @@
         else:
             pay[pl.ds(3 + q, 1), :] = rp
 
-    def u_square(q):
+    def u_square(q, rows):
         mat = mats[q]
-        m = mat["m"]
+        m, n = mat["m"], mat["n"]
         src, first = (late, 0) if q == 2 else (held, q * size)
-        su[...] = jnp.zeros_like(su)
-
-        @pl.loop(0, mat["n"] // 256)
-        def _(c):
-            total = None
-            for half in range(2):
-                c0 = pl.multiple_of(c * 256 + half * 128, 128)
-                g = src[pl.ds(pl.multiple_of(first + (2 * c + half) * m, 128), m), :]
-                t = g * mat["a"][...]
-                bb = mat["b"][:, pl.ds(c0, 128)]
-                s = fold(t * t) * (bb * bb)
-                total = s if total is None else total + s
-            su[...] += total
-
-        pay2[pl.ds(q, 1), :] = jnp.sum(su[...], axis=0, keepdims=True)
+        blocks = n // 128
+
+        def chunk(r, sums):
+            r0 = pl.multiple_of(r * rows, 8)
+            a = mat["a"][pl.ds(r0, rows), :]
+            new = []
+            for c in range(blocks):
+                t = src[pl.ds(pl.multiple_of(first + c * m + r0, 8), rows), :] * a
+                new.append(sums[c] + fold(t * t))
+            return tuple(new)
+
+        sums = lax.fori_loop(0, m // rows, chunk, (jnp.zeros((8, 128), F32),) * blocks)
+        total = None
+        for c in range(blocks):
+            bb = mat["b"][:, c * 128:(c + 1) * 128]
+            s = sums[c] * (bb * bb)
+            total = s if total is None else total + s
+        pay2[pl.ds(q, 1), :] = jnp.sum(total, axis=0, keepdims=True)
 
     rows = md // CHUNKS
     steps = nd // NT * CHUNKS
@@ -346,11 +360,11 @@
     for c in sums:
         c.start()
     for q in range(2):
-        u_square(q)
+        u_square(q, 64)
     for c in sends:
         c.wait()
     new_stats(2)
-    u_square(2)
+    u_square(2, md // 4)
     sums2 = plane_sends(pay2, got2, 4, p2_s, p2_r)
     for c in sums2:
         c.start()
@@ -420,7 +434,7 @@
         def vmem(*arrays):
             return tuple(pltpu.with_memory_space_constraint(v, VM) for v in arrays)
 
-        one = tuple(v.reshape(1, 1) for v in (beta_two, rel_step, clip_thr))
+        one = tuple(lax.ppermute(v.reshape(1, 1), 'data', [(i, (i + 1) % 4) for i in range(4)]) for v in (beta_two, rel_step, clip_thr))
         dims = [(mg, ng), (mg, ng), (md, nd)]
         mm, nn = max(mg, md), max(ng, nd)
         dma = pltpu.SemaphoreType.DMA
@@ -460,7 +474,7 @@
             vmem(*first) + hbm(w_up, w_down) + one, [VM] * len(first) + [HB] * 2 + [pltpu.SMEM] * 3, VM,
             [
                 dma((2,)),
-                VM((md, 128), F32), VM((8, nd), F32), VM((8, 128), F32), VM((8, 128), F32),
+                VM((md, 128), F32), VM((8, nd), F32), VM((8, 128), F32),
                 VM((3, 1, mm), F32), VM((3, 1, mm), F32), VM((3, 1, nn), F32), VM((3, 3, 1, nn), F32),
                 VM((8, 128), F32), VM((7, 8, 128), F32), VM((8, 128), F32), VM((7, 8, 128), F32),
                 dma((3,)), dma((3,)), dma((3, 3)), dma((3, 3)), dma((7,)), dma((7,)), dma((7,)), dma((7,)),

time: 44.9 us -> 46.7 us (1.040)
  starting transfers between devices: 0 us -> 6.29 us
  Pallas kernels: 42 us -> 39.3 us
  between operations: 2.76 us -> 0.85 us
    ppermute x0 -> x3, starting transfers between devices: none -> 6.29 us  [local_program(): lax.ppermute(v.reshape(1, 1), 'data', [(i, (i + 1) % 4) for i in range(4)])]
    pallas_call x3, Pallas kernels: 42 us -> 39.3 us  [call(): pl.pallas_call(functools.partial(kernel, dims), out_shape=outs, in_specs=...]
  transfers between devices with their start and end apart: 0 -> 3, of which waited for: 0 -> 0; matrix products, arithmetic and copies ran while one was open for 0% -> 0% of each run, Pallas kernels for 0% -> 34%
where the time goes in v7:
time: 46.7 us; the launch traced here: 46.5 us
  Pallas kernels  39.3 us (84%)
  starting transfers between devices  6.29 us (13%)
  between operations  0.85 us (2%)
    pallas_call x3, Pallas kernels, call(): pl.pallas_call(functools.partial(kernel, dims), out_shape=outs, in_specs=...  39.3 us
    ppermute x3, starting transfers between devices, local_program(): lax.ppermute(v.reshape(1, 1), 'data', [(i, (i + 1) % 4) for i in range(4)])  6.29 us
  transfers between devices with their start and end apart: 3, of which 0 were waited for; matrix products, arithmetic and copies ran while one was open for 0% of the time, Pallas kernels for 34%

profile of v7, /device:TPU:0, one launch (start us, length us, event | category | flops | bytes accessed | tf_op | source)
XLA Modules:
  0.0 46.5 jit_solution(182571335882284530)
XLA Ops:
  0.6 3.1 %collective-permute-start = (f32[1,1]{1,0:T(1,128)}, f32[1,1]{1,0:T(1,128)}, u32[]{:S(2)}, u32[]{:S(2)}) collective-permute-start(f32[1,1]{1,0:T(1,128)} %bitcast), channel_id=1, source_target_pairs={{0,8},{8,16},{16,24},{24,0},{1,9},{9,17},{17,25},{25,1},{2,10},{10... | collective-permute-start | bytes 20 | tf_op jit(solution)/shard_map/ppermute | solution.py:437
  3.8 1.6 %collective-permute-start.1 = (f32[1,1]{1,0:T(1,128)}, f32[1,1]{1,0:T(1,128)}, u32[]{:S(2)}, u32[]{:S(2)}) collective-permute-start(f32[1,1]{1,0:T(1,128)} %bitcast.1), channel_id=1, source_target_pairs={{0,8},{8,16},{16,24},{24,0},{1,9},{9,17},{17,25},{25,1},{2,10},{10... | collective-permute-start | bytes 20 | tf_op jit(solution)/shard_map/ppermute | solution.py:437
  5.4 1.6 %collective-permute-start.2 = (f32[1,1]{1,0:T(1,128)}, f32[1,1]{1,0:T(1,128)}, u32[]{:S(2)}, u32[]{:S(2)}) collective-permute-start(f32[1,1]{1,0:T(1,128)} %bitcast.2), channel_id=1, source_target_pairs={{0,8},{8,16},{16,24},{24,0},{1,9},{9,17},{17,25},{25,1},{2,10},{10... | collective-permute-start | bytes 20 | tf_op jit(solution)/shard_map/ppermute | solution.py:437
  6.9 15.6 %dot_kernel.1 = (f32[22528,128]{1,0:T(8,128)S(1)}, bf16[1408,2048]{1,0:T(8,128)(2,1)S(1)}, bf16[2048,1024]{1,0:T(8,128)(2,1)S(1)}, f32[512,2816]{1,0:T(8,128)S(1...) custom-call(bf16[2048,512]{1,0:T(8,128)(2,1)} %x.1, ...), custom_call_target="tpu_custom_call" | custom-call | tf_op jit(solution)/shard_map/dot_kernel/pallas_call | solution.py:443
  22.6 0.0 collective-permute-done.b2
  22.6 0.0 collective-permute-done.1.rel
  22.6 0.0 collective-permute-done.2.clip
  22.6 17.5 %exchange_kernel.1 = (f32[11264,128]{1,0:T(8,128)S(1)}, f32[512,2816]{1,0:T(8,128)S(1)}, f32[1408,1024]{1,0:T(8,128)S(1)}, f32[512,128]{1,0:T(8,128)S(1)}, f32[5...) custom-call(f32[22528,128]{1,0:T(8,128)S(1)} %get-tuple-element.35.h, ...), custom_call_target="tpu_custom_call" | custom-call | tf_op jit(solution)/shard_map/exchange_kernel/pallas_call | solution.py:443
  40.1 6.2 %write_kernel.1 = (f32[512,2816]{1,0:T(8,128)}, f32[512,2816]{1,0:T(8,128)}, f32[1408,1024]{1,0:T(8,128)}, f32[512]{0:T(512)}, f32[2816]{0:T(1024)}, /*index=5*/...) custom-call(f32[22528,128]{1,0:T(8,128)S(1)} %get-tuple-element.35.held, ...), custom_call_target="tpu_custom_call" | custom-call | tf_op jit(solution)/shard_map/write_kernel/pallas_call | solution.py:443
Async XLA Ops:
  0.6 21.9 %collective-permute-start = (f32[1,1]{1,0:T(1,128)}, f32[1,1]{1,0:T(1,128)}, u32[]{:S(2)}, u32[]{:S(2)}) collective-permute-start(f32[1,1]{1,0:T(1,128)} %bitcast), channel_id=1, source_target_pairs={{0,8},{8,16},{16,24},{24,0},{1,9},{9,17},{17,25},{25,1},{2,10},{10... | collective-permute-start | bytes 20 | tf_op jit(solution)/shard_map/ppermute | solution.py:437
  3.8 18.8 %collective-permute-start.1 = (f32[1,1]{1,0:T(1,128)}, f32[1,1]{1,0:T(1,128)}, u32[]{:S(2)}, u32[]{:S(2)}) collective-permute-start(f32[1,1]{1,0:T(1,128)} %bitcast.1), channel_id=1, source_target_pairs={{0,8},{8,16},{16,24},{24,0},{1,9},{9,17},{17,25},{25,1},{2,10},{10... | collective-permute-start | bytes 20 | tf_op jit(solution)/shard_map/ppermute | solution.py:437
  5.4 17.2 %collective-permute-start.2 = (f32[1,1]{1,0:T(1,128)}, f32[1,1]{1,0:T(1,128)}, u32[]{:S(2)}, u32[]{:S(2)}) collective-permute-start(f32[1,1]{1,0:T(1,128)} %bitcast.2), channel_id=1, source_target_pairs={{0,8},{8,16},{16,24},{24,0},{1,9},{9,17},{17,25},{25,1},{2,10},{10... | collective-permute-start | bytes 20 | tf_op jit(solution)/shard_map/ppermute | solution.py:437

commit v8 on v7

--- a/solution.py
+++ b/solution.py
@@ -434,7 +434,7 @@
         def vmem(*arrays):
             return tuple(pltpu.with_memory_space_constraint(v, VM) for v in arrays)
 
-        one = tuple(lax.ppermute(v.reshape(1, 1), 'data', [(i, (i + 1) % 4) for i in range(4)]) for v in (beta_two, rel_step, clip_thr))
+        one = tuple(v.reshape(1, 1) for v in (beta_two, rel_step, clip_thr))
         dims = [(mg, ng), (mg, ng), (md, nd)]
         mm, nn = max(mg, md), max(ng, nd)
         dma = pltpu.SemaphoreType.DMA

time: 46.7 us -> 42 us (0.90)
  starting transfers between devices: 6.29 us -> 0 us
  between operations: 0.85 us -> 2.76 us
    ppermute x3 -> x0, starting transfers between devices: 6.29 us -> none  [local_program(): lax.ppermute(v.reshape(1, 1), 'data', [(i, (i + 1) % 4) for i in range(4)])]
  transfers between devices with their start and end apart: 3 -> 0, of which waited for: 0 -> 0; matrix products, arithmetic and copies ran while one was open for 0% -> 0% of each run, Pallas kernels for 34% -> 0%
where the time goes in v8:
time: 42 us; the launch traced here: 41.8 us
  Pallas kernels  39 us (93%)
  between operations  2.76 us (7%)
    pallas_call x3, Pallas kernels, call(): pl.pallas_call(functools.partial(kernel, dims), out_shape=outs, in_specs=...  39 us

profile of v8, /device:TPU:0, one launch (start us, length us, event | category | flops | bytes accessed | tf_op | source)
XLA Modules:
  0.0 41.8 jit_solution(7814412650071871714)
XLA Ops:
  2.6 15.6 %dot_kernel.1 = (f32[22528,128]{1,0:T(8,128)S(1)}, bf16[1408,2048]{1,0:T(8,128)(2,1)S(1)}, bf16[2048,1024]{1,0:T(8,128)(2,1)S(1)}, f32[512,2816]{1,0:T(8,128)S(1...) custom-call(bf16[2048,512]{1,0:T(8,128)(2,1)} %x.1, ...), custom_call_target="tpu_custom_call" | custom-call | tf_op jit(solution)/shard_map/dot_kernel/pallas_call | solution.py:443
  18.2 17.2 %exchange_kernel.1 = (f32[11264,128]{1,0:T(8,128)S(1)}, f32[512,2816]{1,0:T(8,128)S(1)}, f32[1408,1024]{1,0:T(8,128)S(1)}, f32[512,128]{1,0:T(8,128)S(1)}, f32[5...) custom-call(f32[22528,128]{1,0:T(8,128)S(1)} %get-tuple-element.35.h, ...), custom_call_target="tpu_custom_call" | custom-call | tf_op jit(solution)/shard_map/exchange_kernel/pallas_call | solution.py:443
  35.4 6.2 %write_kernel.1 = (f32[512,2816]{1,0:T(8,128)}, f32[512,2816]{1,0:T(8,128)}, f32[1408,1024]{1,0:T(8,128)}, f32[512]{0:T(512)}, f32[2816]{0:T(1024)}, /*index=5*/...) custom-call(f32[22528,128]{1,0:T(8,128)S(1)} %get-tuple-element.35.held, ...), custom_call_target="tpu_custom_call" | custom-call | tf_op jit(solution)/shard_map/write_kernel/pallas_call | solution.py:443

commit v9 on v8

--- a/solution.py
+++ b/solution.py
@@ -106,9 +106,9 @@
         before[u].append(h_copy(k).wait)
         for part in range(2):
             beside[u + part].append(lambda k=k, part=part: h_turn(k, part))
-    before[head(11)].append(bigs[0].start)
-    before[head(14)].append(bigs[1].start)
-    w0 = head(19)
+    before[head(13)].append(bigs[0].start)
+    before[head(15)].append(bigs[1].start)
+    w0 = head(20)
     before[w0].append(bigs[0].wait)
     span = n_units - w0
     for c in range(n // 128):
@@ -198,7 +198,7 @@
     wuh, wdh,
     b2, rel, clip,
     late, wu, wd, a_g, a_u, a_d, b_g, b_u, b_d, r_g, c_g, r_u, c_u, r_d, c_d,
-    w_sem, rs_d, cs_d, sw, rsend, rrecv, csend, crecv, pay, got, pay2, got2, r1s, r1r, c1s, c1r, p_s, p_r, p2_s, p2_r,
+    w_sem, rs_d, cs_d, rsend, rrecv, csend, crecv, pay, got, pay2, got2, r1s, r1r, c1s, c1r, p_s, p_r, p2_s, p2_r,
 ):
     col = lax.axis_index("col")
     row = lax.axis_index("row")
@@ -225,17 +225,22 @@
     pay[...] = jnp.zeros_like(pay)
     pay2[...] = jnp.zeros_like(pay2)
 
-    def w_square(q, w):
+    def w_square(q, w, rows):
         m, n = dims[q]
-        sw[...] = jnp.zeros_like(sw)
-
-        @pl.loop(0, n // 256)
-        def _(c):
-            c0 = pl.multiple_of(c * 256, 256)
-            a, b = w[:, pl.ds(c0, 128)], w[:, pl.ds(c0 + 128, 128)]
-            sw[...] += fold(a * a) + fold(b * b)
-
-        pay[pl.ds(q, 1), :] = jnp.sum(sw[...], axis=0, keepdims=True)
+
+        def chunk(r, sums):
+            rr = pl.ds(pl.multiple_of(r * rows, 8), rows)
+            new = []
+            for c in range(n // 128):
+                v = w[rr, c * 128:(c + 1) * 128]
+                new.append(sums[c] + fold(v * v))
+            return tuple(new)
+
+        sums = lax.fori_loop(0, m // rows, chunk, (jnp.zeros((8, 128), F32),) * (n // 128))
+        total = sums[0]
+        for v in sums[1:]:
+            total = total + v
+        pay[pl.ds(q, 1), :] = jnp.sum(total, axis=0, keepdims=True)
 
     def first_sends(q):
         mat = mats[q]
@@ -354,8 +359,8 @@
         new_stats(q)
     for c in loads:
         c.wait()
-    w_square(1, wu)
-    w_square(2, wd)
+    w_square(1, wu, 64)
+    w_square(2, wd, md // 8)
     sums = plane_sends(pay, got, 5, p_s, p_r)
     for c in sums:
         c.start()
@@ -364,7 +369,7 @@
     for c in sends:
         c.wait()
     new_stats(2)
-    u_square(2, md // 4)
+    u_square(2, md // 8)
     sums2 = plane_sends(pay2, got2, 4, p2_s, p2_r)
     for c in sums2:
         c.start()
@@ -474,7 +479,7 @@
             vmem(*first) + hbm(w_up, w_down) + one, [VM] * len(first) + [HB] * 2 + [pltpu.SMEM] * 3, VM,
             [
                 dma((2,)),
-                VM((md, 128), F32), VM((8, nd), F32), VM((8, 128), F32),
+                VM((md, 128), F32), VM((8, nd), F32),
                 VM((3, 1, mm), F32), VM((3, 1, mm), F32), VM((3, 1, nn), F32), VM((3, 3, 1, nn), F32),
                 VM((8, 128), F32), VM((7, 8, 128), F32), VM((8, 128), F32), VM((7, 8, 128), F32),
                 dma((3,)), dma((3,)), dma((3, 3)), dma((3, 3)), dma((7,)), dma((7,)), dma((7,)), dma((7,)),

time: 42 us -> 41.3 us (0.983)
  Pallas kernels: 39 us -> 38.3 us
    pallas_call x3, Pallas kernels: 39 us -> 38.3 us  [call(): pl.pallas_call(functools.partial(kernel, dims), out_shape=outs, in_specs=...]
where the time goes in v9:
time: 41.3 us; the launch traced here: 41.1 us
  Pallas kernels  38.3 us (93%)
  between operations  2.76 us (7%)
    pallas_call x3, Pallas kernels, call(): pl.pallas_call(functools.partial(kernel, dims), out_shape=outs, in_specs=...  38.3 us

profile of v9, /device:TPU:0, one launch (start us, length us, event | category | flops | bytes accessed | tf_op | source)
XLA Modules:
  0.0 41.1 jit_solution(3923495116285191918)
XLA Ops:
  2.6 15.5 %dot_kernel.1 = (f32[22528,128]{1,0:T(8,128)S(1)}, bf16[1408,2048]{1,0:T(8,128)(2,1)S(1)}, bf16[2048,1024]{1,0:T(8,128)(2,1)S(1)}, f32[512,2816]{1,0:T(8,128)S(1...) custom-call(bf16[2048,512]{1,0:T(8,128)(2,1)} %x.1, ...), custom_call_target="tpu_custom_call" | custom-call | tf_op jit(solution)/shard_map/dot_kernel/pallas_call | solution.py:448
  18.1 16.6 %exchange_kernel.1 = (f32[11264,128]{1,0:T(8,128)S(1)}, f32[512,2816]{1,0:T(8,128)S(1)}, f32[1408,1024]{1,0:T(8,128)S(1)}, f32[512,128]{1,0:T(8,128)S(1)}, f32[5...) custom-call(f32[22528,128]{1,0:T(8,128)S(1)} %get-tuple-element.35.h, ...), custom_call_target="tpu_custom_call" | custom-call | tf_op jit(solution)/shard_map/exchange_kernel/pallas_call | solution.py:448
  34.7 6.2 %write_kernel.1 = (f32[512,2816]{1,0:T(8,128)}, f32[512,2816]{1,0:T(8,128)}, f32[1408,1024]{1,0:T(8,128)}, f32[512]{0:T(512)}, f32[2816]{0:T(1024)}, /*index=5*/...) custom-call(f32[22528,128]{1,0:T(8,128)S(1)} %get-tuple-element.35.held, ...), custom_call_target="tpu_custom_call" | custom-call | tf_op jit(solution)/shard_map/write_kernel/pallas_call | solution.py:448

commit v10 on v9

--- a/solution.py
+++ b/solution.py
@@ -163,7 +163,7 @@
                     for z in range(2):
                         xt[pl.ds(z * 256, 256), pl.ds(k * KB, KB)] = xs[k, :, pl.ds(z * 256, 256)].T
                         pltpu.matmul_push_rhs(rhs(0, k), staging_register=k % 2, mxu_index=z)
-                    if k % 2 and k // 2 + 1 < RING:
+                    if k % 2 == 0 and k // 2 + 1 < RING:
                         d_copy(k // 2 + 1).start()
                     if k == nk - 1 and unit_tile[1][0] == 1:
                         d_copy(1).wait()

time: 41.3 us -> 41.1 us (level)
  no operation moved by 1% of the time
where the time goes in v10:
time: 41.1 us; the launch traced here: 40.9 us
  Pallas kernels  38.2 us (93%)
  between operations  2.76 us (7%)
    pallas_call x3, Pallas kernels, call(): pl.pallas_call(functools.partial(kernel, dims), out_shape=outs, in_specs=...  38.2 us

profile of v10, /device:TPU:0, one launch (start us, length us, event | category | flops | bytes accessed | tf_op | source)
XLA Modules:
  0.0 40.9 jit_solution(6261143764061775853)
XLA Ops:
  2.6 15.3 %dot_kernel.1 = (f32[22528,128]{1,0:T(8,128)S(1)}, bf16[1408,2048]{1,0:T(8,128)(2,1)S(1)}, bf16[2048,1024]{1,0:T(8,128)(2,1)S(1)}, f32[512,2816]{1,0:T(8,128)S(1...) custom-call(bf16[2048,512]{1,0:T(8,128)(2,1)} %x.1, ...), custom_call_target="tpu_custom_call" | custom-call | tf_op jit(solution)/shard_map/dot_kernel/pallas_call | solution.py:448
  17.9 16.6 %exchange_kernel.1 = (f32[11264,128]{1,0:T(8,128)S(1)}, f32[512,2816]{1,0:T(8,128)S(1)}, f32[1408,1024]{1,0:T(8,128)S(1)}, f32[512,128]{1,0:T(8,128)S(1)}, f32[5...) custom-call(f32[22528,128]{1,0:T(8,128)S(1)} %get-tuple-element.35.h, ...), custom_call_target="tpu_custom_call" | custom-call | tf_op jit(solution)/shard_map/exchange_kernel/pallas_call | solution.py:448
  34.5 6.2 %write_kernel.1 = (f32[512,2816]{1,0:T(8,128)}, f32[512,2816]{1,0:T(8,128)}, f32[1408,1024]{1,0:T(8,128)}, f32[512]{0:T(512)}, f32[2816]{0:T(1024)}, /*index=5*/...) custom-call(f32[22528,128]{1,0:T(8,128)S(1)} %get-tuple-element.35.held, ...), custom_call_target="tpu_custom_call" | custom-call | tf_op jit(solution)/shard_map/write_kernel/pallas_call | solution.py:448

commit v11 on v10

--- a/solution.py
+++ b/solution.py
@@ -256,23 +256,18 @@
 
     def first_reduce(q):
         mat = mats[q]
-        csend[q, :, pl.ds(0, mat["n"])] = jnp.sum(mat["cs"][...], axis=0, keepdims=True)
         for b in range(mat["m"] // 128):
             t = mat["rs"][pl.ds(b * 128, 128), :].T
             rsend[q, :, pl.ds(b * 128, 128)] = jnp.sum(t, axis=0, keepdims=True)
-
-    def new_stats(q):
+        csend[q, :, pl.ds(0, mat["n"])] = jnp.sum(mat["cs"][...], axis=0, keepdims=True)
+
+    def new_rows(q):
         mat = mats[q]
-        m, n = mat["m"], mat["n"]
+        m = mat["m"]
         beta = b2[0, 0]
         rsum = rsend[q, :, pl.ds(0, m)] + rrecv[q, :, pl.ds(0, m)]
         r_new = beta * ro[q, :, pl.ds(0, m)] + (1.0 - beta) * (rsum * (1.0 / mat["nt"]) + EPS_SQ)
         mat["r"][...] = r_new
-        csum = (csend[q, :, pl.ds(0, n)] + crecv[q, 0, :, pl.ds(0, n)]) + (
-            crecv[q, 1, :, pl.ds(0, n)] + crecv[q, 2, :, pl.ds(0, n)])
-        c_new = beta * co[q, :, pl.ds(0, n)] + (1.0 - beta) * (csum * (1.0 / mat["mt"]) + EPS_SQ)
-        mat["c"][...] = c_new
-        mat["b"][...] = lax.rsqrt(c_new)
         alpha = lax.rsqrt(r_new)
         rp = r_new[:, :128]
         for b in range(m // 128):
@@ -285,7 +280,17 @@
         else:
             pay[pl.ds(3 + q, 1), :] = rp
 
-    def u_square(q, rows):
+    def new_cols(q):
+        mat = mats[q]
+        n = mat["n"]
+        beta = b2[0, 0]
+        csum = (csend[q, :, pl.ds(0, n)] + crecv[q, 0, :, pl.ds(0, n)]) + (
+            crecv[q, 1, :, pl.ds(0, n)] + crecv[q, 2, :, pl.ds(0, n)])
+        c_new = beta * co[q, :, pl.ds(0, n)] + (1.0 - beta) * (csum * (1.0 / mat["mt"]) + EPS_SQ)
+        mat["c"][...] = c_new
+        mat["b"][...] = lax.rsqrt(c_new)
+
+    def u_square(q, rows, waits=()):
         mat = mats[q]
         m, n = mat["m"], mat["n"]
         src, first = (late, 0) if q == 2 else (held, q * size)
@@ -301,6 +306,9 @@
             return tuple(new)
 
         sums = lax.fori_loop(0, m // rows, chunk, (jnp.zeros((8, 128), F32),) * blocks)
+        for c in waits:
+            c.wait()
+        new_cols(q)
         total = None
         for c in range(blocks):
             bb = mat["b"][:, c * 128:(c + 1) * 128]
@@ -356,7 +364,7 @@
         c.wait()
     pay[pl.ds(0, 1), :] = jnp.sum(sw_g[...], axis=0, keepdims=True)
     for q in range(2):
-        new_stats(q)
+        new_rows(q)
     for c in loads:
         c.wait()
     w_square(1, wu, 64)
@@ -366,10 +374,9 @@
         c.start()
     for q in range(2):
         u_square(q, 64)
-    for c in sends:
-        c.wait()
-    new_stats(2)
-    u_square(2, md // 8)
+    sends[0].wait()
+    new_rows(2)
+    u_square(2, md // 8, sends[1:])
     sums2 = plane_sends(pay2, got2, 4, p2_s, p2_r)
     for c in sums2:
         c.start()

time: 41.1 us -> 41.2 us (level)
  no operation moved by 1% of the time
where the time goes in v11:
time: 41.2 us; the launch traced here: 41 us
  Pallas kernels  38.2 us (93%)
  between operations  2.76 us (7%)
    pallas_call x3, Pallas kernels, call(): pl.pallas_call(functools.partial(kernel, dims), out_shape=outs, in_specs=...  38.2 us

profile of v11, /device:TPU:0, one launch (start us, length us, event | category | flops | bytes accessed | tf_op | source)
XLA Modules:
  0.0 41.0 jit_solution(3261575093944978496)
XLA Ops:
  2.6 15.3 %dot_kernel.1 = (f32[22528,128]{1,0:T(8,128)S(1)}, bf16[1408,2048]{1,0:T(8,128)(2,1)S(1)}, bf16[2048,1024]{1,0:T(8,128)(2,1)S(1)}, f32[512,2816]{1,0:T(8,128)S(1...) custom-call(bf16[2048,512]{1,0:T(8,128)(2,1)} %x.1, ...), custom_call_target="tpu_custom_call" | custom-call | tf_op jit(solution)/shard_map/dot_kernel/pallas_call | solution.py:455
  17.9 16.7 %exchange_kernel.1 = (f32[11264,128]{1,0:T(8,128)S(1)}, f32[512,2816]{1,0:T(8,128)S(1)}, f32[1408,1024]{1,0:T(8,128)S(1)}, f32[512,128]{1,0:T(8,128)S(1)}, f32[5...) custom-call(f32[22528,128]{1,0:T(8,128)S(1)} %get-tuple-element.35.h, ...), custom_call_target="tpu_custom_call" | custom-call | tf_op jit(solution)/shard_map/exchange_kernel/pallas_call | solution.py:455
  34.6 6.2 %write_kernel.1 = (f32[512,2816]{1,0:T(8,128)}, f32[512,2816]{1,0:T(8,128)}, f32[1408,1024]{1,0:T(8,128)}, f32[512]{0:T(512)}, f32[2816]{0:T(1024)}, /*index=5*/...) custom-call(f32[22528,128]{1,0:T(8,128)S(1)} %get-tuple-element.35.held, ...), custom_call_target="tpu_custom_call" | custom-call | tf_op jit(solution)/shard_map/write_kernel/pallas_call | solution.py:455
